TPU v7x, 128 devices: a whole 4x4x4 slice. The times are simulated.
128 devices in a mesh: rep: 16 (over x_hi, z, core), tp: 8 (over x_lo, y).
Axes of the slice: x: 4 (x_hi: 2, x_lo: 2; x = x_hi * 2 + x_lo), y: 4, z: 4, core: 2. Of those that a mesh axis runs over, the one named last changes fastest.
Arguments:
- hidden: bfloat16 [64, 4608], P('rep'), may hold values from -6 to 6
- positions: int32 [64], P('rep'), may hold values from 1 to 1023
- key_cache: bfloat16 [64, 16, 1024, 128], P('rep', 'tp'), may hold values from -6 to 6
- value_cache: bfloat16 [64, 16, 1024, 128], P('rep', 'tp'), may hold values from -6 to 6
- norm_gain: float32 [4608], replicated, may hold values from 0.1 to 1.9
- q_proj: bfloat16 [4096, 4608], P(('rep', 'tp')), may hold values from -0.09375 to 0.09375
- k_proj: bfloat16 [2048, 4608], P(('rep', 'tp')), may hold values from -0.09375 to 0.09375
- v_proj: bfloat16 [2048, 4608], P(('rep', 'tp')), may hold values from -0.09375 to 0.09375
- o_proj: bfloat16 [4608, 4096], P(('rep', 'tp')), may hold values from -0.09375 to 0.09375
- post_gain: float32 [4608], P('tp'), may hold values from 0.1 to 1.9
Outputs:
- joined_qkv: bfloat16 [4608, 8192], P(None, 'tp')
- wo_heads: bfloat16 [4096, 4608], P('tp')
- attn_out: bfloat16 [64, 4608], P('rep', 'tp')
All inputs are finite; a program needn't handle non-finite values.
Results may differ from a plain program's by a relative error of at most 0.008.
Values may be sent and summed in bfloat16 or wider, within the bound.
A program may use at most 128 MiB of HBM per device.

v0:
```python
import jax
import jax.numpy as jnp
from jax import lax
from jax.sharding import PartitionSpec as P

score_scale = 144.0 ** (-0.5)
soft_cap = 50.0


def side_by_side(arrays, axis, dim, along):
    widths = [a.shape[along] for a in arrays]
    both = jnp.concatenate(arrays, axis=along)
    result = lax.all_gather(both, axis, axis=dim, tiled=True)
    return tuple(jnp.split(result, [sum(widths[:k]) for k in range(1, len(widths))], axis=along))


def sent_to_all(shard, axis):
    size = lax.axis_size(axis)
    return lax.all_to_all(
        jnp.broadcast_to(shard[None], (size, *shard.shape)), axis, 0, 0, tiled=True
    )


def over_copies(shard, axis):
    return sent_to_all(shard, axis).sum(axis=0)


def rms_scale(values, gain):
    mean_square = jnp.mean(values * values, axis=-1, keepdims=True)
    return values * lax.rsqrt(mean_square + 1e-06) * gain


def rotate(values, positions):
    half = values.shape[-1] // 2
    freq = 10000.0 ** (-2.0 * jnp.arange(half, dtype=jnp.float32) / values.shape[-1])
    angle = positions.astype(jnp.float32)[:, None] * freq[None, :]
    cosine = jnp.cos(angle)[:, None, :]
    sine = jnp.sin(angle)[:, None, :]
    first = values[..., :half]
    second = values[..., half:]
    return jnp.concatenate(
        [first * cosine - second * sine, second * cosine + first * sine], axis=-1
    )


def body(
    hidden, positions, key_cache, value_cache, norm_gain, q_proj, k_proj, v_proj, o_proj, post_gain
):
    tp_count = lax.axis_size("tp")
    replica_count = lax.axis_size("rep")
    per_tp = replica_count // tp_count
    model_width = hidden.shape[1]
    stacked = side_by_side((q_proj[None], k_proj[None], v_proj[None]), "rep", 0, 1)
    shaped = [matrix.reshape((tp_count, per_tp, 1) + matrix.shape[1:]) for matrix in stacked]
    arrived = (
        lax.all_to_all(shaped[0], "tp", split_axis=0, concat_axis=2, tiled=True),
        lax.all_to_all(shaped[1], "tp", split_axis=0, concat_axis=2, tiled=True),
        lax.all_to_all(shaped[2], "tp", split_axis=0, concat_axis=2, tiled=True),
    )
    head_block = [matrix.reshape(-1, model_width) for matrix in arrived]
    joined_block = jnp.transpose(jnp.concatenate(head_block, axis=0))
    split_cols = o_proj.reshape(o_proj.shape[0], tp_count, -1)
    rows_of_group = lax.all_to_all(split_cols, "tp", split_axis=1, concat_axis=0, tiled=True)
    complete_rows = lax.all_gather(rows_of_group, "rep", axis=0, tiled=True)
    out_block = jnp.transpose(complete_rows.reshape(model_width, -1))
    batch, kv_local, length, head_dim = key_cache.shape
    q_width = head_block[0].shape[0]
    kv_width = head_block[1].shape[0]
    q_local = q_width // head_dim
    group = q_local // kv_local
    normed = rms_scale(hidden.astype(jnp.float32), norm_gain).astype(jnp.bfloat16)
    query_key_value_projected = jnp.dot(normed, joined_block, preferred_element_type=jnp.float32)
    query = query_key_value_projected[:, :q_width].reshape(batch, q_local, head_dim)
    keys_new = query_key_value_projected[:, q_width : q_width + kv_width].reshape(
        batch, kv_local, head_dim
    )
    values_new = query_key_value_projected[:, q_width + kv_width :].reshape(
        batch, kv_local, head_dim
    )
    query_rot = rotate(query, positions).astype(jnp.bfloat16)
    rotated_keys = rotate(keys_new, positions).astype(jnp.bfloat16)
    values_rot = values_new.astype(jnp.bfloat16)
    grouped_heads = query_rot.reshape(batch, kv_local, group, head_dim)
    scores = (
        jnp.einsum("bkgd,bkld->bkgl", grouped_heads, key_cache, preferred_element_type=jnp.float32)
        * score_scale
    )
    capped = soft_cap * jnp.tanh(scores / soft_cap)
    valid = jnp.arange(length, dtype=jnp.int32)[None, :] < positions[:, None]
    weight_raw = jnp.where(valid[:, None, None, :], jnp.exp(capped), 0.0)
    self_score = (
        jnp.einsum("juzy,juy->juz", grouped_heads, rotated_keys, preferred_element_type=jnp.float32)
        * score_scale
    )
    self_raw = jnp.exp(soft_cap * jnp.tanh(self_score / soft_cap))
    denom = jnp.sum(weight_raw, axis=-1) + self_raw
    weights = (weight_raw / denom[..., None]).astype(jnp.bfloat16)
    self_weight = (self_raw / denom).astype(jnp.bfloat16)
    attention = jnp.einsum(
        "bkgl,bkld->bkgd", weights, value_cache, preferred_element_type=jnp.float32
    )
    attention = (
        attention
        + self_weight.astype(jnp.float32)[..., None] * values_rot.astype(jnp.float32)[:, :, None, :]
    )
    attention = attention.reshape(batch, q_width).astype(jnp.bfloat16)
    partial_out = jnp.dot(attention, out_block, preferred_element_type=jnp.float32)
    width_local = post_gain.shape[0]
    total = over_copies(partial_out, "tp")
    multiplier = lax.rsqrt(jnp.mean(total * total, axis=1) + 1e-06)
    share = lax.dynamic_slice_in_dim(total, lax.axis_index("tp") * width_local, width_local, 1)
    result = share * multiplier[:, None] * post_gain
    return (joined_block, out_block, result.astype(jnp.bfloat16))


def solution(mesh):
    in_specs = (
        P("rep", None),
        P("rep"),
        P("rep", "tp", None, None),
        P("rep", "tp", None, None),
        P(),
        P(("rep", "tp"), None),
        P(("rep", "tp"), None),
        P(("rep", "tp"), None),
        P(("rep", "tp"), None),
        P("tp"),
    )
    out_specs = (P(None, "tp"), P("tp", None), P("rep", "tp"))
    return jax.shard_map(body, mesh=mesh, in_specs=in_specs, out_specs=out_specs, check_vma=False)
```

profile of v0, /device:TPU:1, one launch (start us, length us, event | category | flops | bytes accessed | tf_op | source)
XLA Modules:
  0.0 273.7 jit_solution(10888830061418222537)
XLA Ops:
  7.2 2.1 pad_maximum_fusion.2
  9.4 1.1 copy.57
  10.6 12.5 %all_to_all.68 = bf16[36,8,512]{2,0,1:T(8,128)(2,1)S(1)} all-to-all(bf16[36,8,512]{2,0,1:T(8,128)(2,1)S(1)} %copy.50), channel_id=1, replica_groups=mesh['rep'=16,'tp'=8] {'tp'}, dimensions={1} | all-to-all | bytes 589824 | tf_op jit(solution)/shard_map/all_to_all | solution.py:63
  23.1 0.8 all_to_all.61
  23.9 68.0 %all-gather.3.cloned.1.call-done = bf16[16,64,4608]{2,1,0:T(8,128)(2,1)} async-done(((bf16[1,64,4608]{2,1,0:T(8,128)(2,1)}), bf16[16,64,4608]{2,1,0:T(8,128)(2,1)}) %all-gather.3.cloned.1.call-update) | async-done | bytes 9437200 | tf_op jit(solution)/shard_map/all_gather | solution.py:13
  91.9 4.1 %fusion.22 = (bf16[16,16,4608]{2,1,0:T(8,128)(2,1)S(1)}, bf16[16,16,4608]{2,1,0:T(8,128)(2,1)}) fusion(bf16[16,64,4608]{2,1,0:T(8,128)(2,1)} %all-gather.3.cloned.1.call-done), kind=kLoop, calls=%fused_computation.45 | loop fusion | bytes 9437184 | tf_op jit(solution)/shard_map/split | solution.py:14
  96.0 35.7 %all_to_all.69 = bf16[8,2,1,16,4608]{4,3,1,2,0:T(8,128)(2,1)} all-to-all(bf16[8,2,1,16,4608]{4,3,1,2,0:T(8,128)(2,1)S(1)} %bitcast.60), channel_id=1, replica_groups=mesh['rep'=16,'tp'=8] {'tp'}, dimensions={0} | all-to-all | bytes 4718592 | tf_op jit(solution)/shard_map/all_to_all | solution.py:57
  131.7 4.4 %all-to-all-start.2 = ((bf16[8,2,1,16,4608]{4,3,1,2,0:T(8,128)(2,1)}), bf16[8,2,1,16,4608]{4,3,1,2,0:T(8,128)(2,1)}, u32[]{:S(2)}, u32[]{:S(2)}) async-start(bf16[8,2,1,16,4608]{4,3,1,2,0:T(8,128)(2,1)} %bitcast.59), calls=%async_computation.2 | async-start | bytes 4718592 | tf_op jit(solution)/shard_map/all_to_all | solution.py:58
  136.1 4.9 %split.12 = bf16[16,32,4608]{2,1,0:T(8,128)(2,1)} slice(bf16[16,64,4608]{2,1,0:T(8,128)(2,1)} %all-gather.3.cloned.1.call-done), slice={[0:16], [0:32], [0:4608]} | slice | bytes 9437184 | tf_op jit(solution)/shard_map/split | solution.py:14
  141.0 27.0 %all-to-all-done.2 = bf16[8,2,1,16,4608]{4,3,1,2,0:T(8,128)(2,1)} async-done(((bf16[8,2,1,16,4608]{4,3,1,2,0:T(8,128)(2,1)}), bf16[8,2,1,16,4608]{4,3,1,2,0:T(8,128)(2,1)}, u32[]{:S(2)}, u32[]{:S(2)}) %all-to-all-start.2) | async-done | bytes 2359328 | tf_op jit(solution)/shard_map/all_to_all | solution.py:58
  168.0 4.7 %all-to-all-start = ((bf16[8,2,1,32,4608]{4,3,1,2,0:T(8,128)(2,1)}), bf16[8,2,1,32,4608]{4,3,1,2,0:T(8,128)(2,1)}, u32[]{:S(2)}, u32[]{:S(2)}) async-start(bf16[8,2,1,32,4608]{4,3,1,2,0:T(8,128)(2,1)} %bitcast.52), calls=%async_computation | async-start | bytes 9437184 | tf_op jit(solution)/shard_map/all_to_all | solution.py:56
  173.2 6.6 %copy.53 = bf16[512,4608]{1,0:T(8,128)(2,1)} copy(bf16[512,4608]{0,1:T(8,128)(2,1)} %bitcast.51) | data formatting | bytes 9437184
  179.8 3.2 %copy.47 = bf16[8,2,1,16,4608]{4,3,0,1,2:T(8,128)(2,1)} copy(bf16[8,2,1,16,4608]{4,3,1,2,0:T(8,128)(2,1)} %all_to_all.69) | data formatting | bytes 4718592 | tf_op jit(solution)/shard_map/all_to_all | solution.py:57
  183.0 3.2 %copy.49 = bf16[8,2,1,16,4608]{4,3,0,1,2:T(8,128)(2,1)} copy(bf16[8,2,1,16,4608]{4,3,1,2,0:T(8,128)(2,1)} %all-to-all-done.2) | data formatting | bytes 4718592 | tf_op jit(solution)/shard_map/all_to_all | solution.py:58
  186.2 40.9 %all-to-all-done = bf16[8,2,1,32,4608]{4,3,1,2,0:T(8,128)(2,1)} async-done(((bf16[8,2,1,32,4608]{4,3,1,2,0:T(8,128)(2,1)}), bf16[8,2,1,32,4608]{4,3,1,2,0:T(8,128)(2,1)}, u32[]{:S(2)}, u32[]{:S(2)}) %all-to-all-start) | async-done | bytes 4718624 | tf_op jit(solution)/shard_map/all_to_all | solution.py:56
  227.1 2.9 %copy.45 = bf16[8,2,1,32,4608]{4,3,0,1,2:T(8,128)(2,1)S(1)} copy(bf16[8,2,1,32,4608]{4,3,1,2,0:T(8,128)(2,1)} %all-to-all-done) | data formatting | bytes 9437184 | tf_op jit(solution)/shard_map/all_to_all | solution.py:56
  230.9 3.1 %fusion.2 = f32[4,1024]{1,0:T(4,128)S(1)} fusion(bf16[256,4608]{1,0:T(8,128)(2,1)S(1)} %bitcast.58, bf16[256,4608]{1,0:T(8,128)(2,1)S(1)} %bitcast.56, bf16[512,4608]{1,0:T(8,128)(2,1)S(1)} %bitcast.53, bf16[4,4608]{1,0:T(4,128)(2,1)S(1)} %copy-done.4, f32[4608]{0:T(1024)S(1)} %copy-done.7, f32[4]{0:T(128)S(1)} %add_rsqrt_fusion.1), kind=kOutput, calls=%fused_computation.3 | convolution fusion | flops 66134016 | bytes 9508880 | tf_op jit(solution)/shard_map/dot_general | solution.py:72
  234.6 0.8 fusion.23
  235.4 2.0 fusion.8
  237.4 3.7 %fusion = f32[4,4608]{1,0:T(4,128)S(1)} fusion(bf16[4,512]{1,0:T(4,128)(2,1)S(1)} %convert_element_type.56, bf16[4608,1,512]{2,0,1:T(8,128)(2,1)} %all-gather.5.cloned.1.call-done), kind=kOutput, calls=%fused_computation.1 | convolution fusion | flops 18874368 | bytes 4796416 | tf_op jit(solution)/shard_map/dot_general | solution.py:107
  241.1 0.9 broadcast_in_dim.25
  242.0 3.5 %all-to-all-start.4 = ((f32[8,4,4608]{2,1,0:T(4,128)}), f32[8,4,4608]{2,1,0:T(4,128)S(1)}, u32[]{:S(2)}, u32[]{:S(2)}) async-start(f32[8,4,4608]{2,1,0:T(4,128)} %broadcast_in_dim.25), calls=%async_computation.4 | async-start | bytes 1179648 | tf_op jit(solution)/shard_map/all_to_all | solution.py:19
  245.6 7.7 %fusion.3 = bf16[4608,1024]{0,1:T(8,128)(2,1)} fusion(bf16[256,4608]{1,0:T(8,128)(2,1)} %bitcast.57, bf16[256,4608]{1,0:T(8,128)(2,1)} %bitcast.55, bf16[512,4608]{1,0:T(8,128)(2,1)} %bitcast.54), kind=kLoop, calls=%fused_computation.4 | loop fusion | flops 28311552 | bytes 18874368 | tf_op jit(solution)/shard_map/transpose | solution.py:61
  253.3 12.6 %copy.52 = bf16[4608,1024]{1,0:T(8,128)(2,1)} copy(bf16[4608,1024]{0,1:T(8,128)(2,1)} %fusion.3) | data formatting | bytes 18874368
  (46 shorter events, 3.0 us)
Async XLA Ops:
  7.2 227.4 %copy-start = (bf16[4,2,1024,128]{3,2,1,0:T(8,128)(2,1)S(1)}, bf16[4,2,1024,128]{3,2,1,0:T(8,128)(2,1)}, u32[]{:S(2)}) copy-start(bf16[4,2,1024,128]{3,2,1,0:T(8,128)(2,1)} %param.12) | copy-start | bytes 6291460
  7.2 84.8 %all-gather.3.cloned.1.call-start = ((), (), s32[]{:S(2)}) async-start(), calls=%async_computation.5 | async-start | bytes 10027008 | tf_op jit(solution)/shard_map/all_gather | solution.py:13
  9.3 163.8 %all-gather.5.cloned.1.call-start = ((), (), s32[]{:S(2)}) async-start(), calls=%async_computation.6 | async-start | bytes 5013504 | tf_op jit(solution)/shard_map/all_gather | solution.py:64
  131.7 36.3 %all-to-all-start.2 = ((bf16[8,2,1,16,4608]{4,3,1,2,0:T(8,128)(2,1)}), bf16[8,2,1,16,4608]{4,3,1,2,0:T(8,128)(2,1)}, u32[]{:S(2)}, u32[]{:S(2)}) async-start(bf16[8,2,1,16,4608]{4,3,1,2,0:T(8,128)(2,1)} %bitcast.59), calls=%async_computation.2 | async-start | bytes 4718592 | tf_op jit(solution)/shard_map/all_to_all | solution.py:58
  168.0 4.8 %copy-start.6 = (s32[4]{0:T(128)S(1)}, s32[4]{0:T(128)}, u32[]{:S(2)}) copy-start(s32[4]{0:T(128)} %param.11) | copy-start | bytes 52
  168.0 4.8 %copy-start.4 = (bf16[4,4608]{1,0:T(4,128)(2,1)S(1)}, bf16[4,4608]{1,0:T(4,128)(2,1)}, u32[]{:S(2)}) copy-start(bf16[4,4608]{1,0:T(4,128)(2,1)} %param.10) | copy-start | bytes 110596
  168.0 59.1 %all-to-all-start = ((bf16[8,2,1,32,4608]{4,3,1,2,0:T(8,128)(2,1)}), bf16[8,2,1,32,4608]{4,3,1,2,0:T(8,128)(2,1)}, u32[]{:S(2)}, u32[]{:S(2)}) async-start(bf16[8,2,1,32,4608]{4,3,1,2,0:T(8,128)(2,1)} %bitcast.52), calls=%async_computation | async-start | bytes 9437184 | tf_op jit(solution)/shard_map/all_to_all | solution.py:56
  186.2 43.8 %copy-start.7 = (f32[4608]{0:T(1024)S(1)}, f32[4608]{0:T(1024)}, u32[]{:S(2)}) copy-start(f32[4608]{0:T(1024)} %param.14) | copy-start | bytes 55300
  227.1 3.1 %copy-start.2 = (bf16[8,2,1,16,4608]{4,3,0,1,2:T(8,128)(2,1)S(1)}, bf16[8,2,1,16,4608]{4,3,0,1,2:T(8,128)(2,1)}, u32[]{:S(2)}) copy-start(bf16[8,2,1,16,4608]{4,3,0,1,2:T(8,128)(2,1)} %copy.47) | copy-start | bytes 7077892
  227.1 3.8 %copy-start.3 = (bf16[8,2,1,16,4608]{4,3,0,1,2:T(8,128)(2,1)S(1)}, bf16[8,2,1,16,4608]{4,3,0,1,2:T(8,128)(2,1)}, u32[]{:S(2)}) copy-start(bf16[8,2,1,16,4608]{4,3,0,1,2:T(8,128)(2,1)} %copy.49) | copy-start | bytes 7077892
  230.0 4.1 %copy-start.1 = (bf16[8,2,1,32,4608]{4,3,0,1,2:T(8,128)(2,1)}, bf16[8,2,1,32,4608]{4,3,0,1,2:T(8,128)(2,1)S(1)}, u32[]{:S(2)}) copy-start(bf16[8,2,1,32,4608]{4,3,0,1,2:T(8,128)(2,1)S(1)} %copy.45) | copy-start | bytes 14155780
  242.0 23.9 %all-to-all-start.4 = ((f32[8,4,4608]{2,1,0:T(4,128)}), f32[8,4,4608]{2,1,0:T(4,128)S(1)}, u32[]{:S(2)}, u32[]{:S(2)}) async-start(f32[8,4,4608]{2,1,0:T(4,128)} %broadcast_in_dim.25), calls=%async_computation.4 | async-start | bytes 1179648 | tf_op jit(solution)/shard_map/all_to_all | solution.py:19
  253.3 12.9 %copy-start.5 = (f32[576]{0:T(1024)S(1)}, f32[576]{0:T(1024)}, u32[]{:S(2)}) copy-start(f32[576]{0:T(1024)} %param.19) | copy-start | bytes 6916
Sparse Core Ops, SparseCore 0:
  11.0 80.8 all-gather.2
  94.4 63.6 all-gather.4
where the time goes:
time: 275 us; the launch traced here: 274 us
  waiting for transfers between devices  136 us (49%)
  blocking collectives  48.2 us (18%)
  local copies, waits for them, and re-layouts  41.4 us (15%)
  between operations  14.2 us (5%)
  starting transfers between devices  12.7 us (5%)
  other arithmetic  11.4 us (4%)
  matrix products  9.81 us (4%)
    all_gather x1, waiting for transfers between devices, side_by_side(): result = lax.all_gather(both, axis, axis=dim, tiled=True)  68 us
    all_to_all x1, waiting for transfers between devices, body(): lax.all_to_all(shaped[0], 'tp', split_axis=0, concat_axis=2, tiled=True)  40.9 us
    all_to_all x1, blocking collectives, body(): lax.all_to_all(shaped[1], 'tp', split_axis=0, concat_axis=2, tiled=True)  35.7 us
    all_to_all x1, waiting for transfers between devices, body(): lax.all_to_all(shaped[2], 'tp', split_axis=0, concat_axis=2, tiled=True)  27 us
    unnamed x19, local copies, waits for them, and re-layouts  21.2 us
    all_to_all x1, blocking collectives, body(): lax.all_to_all(split_cols, 'tp', split_axis=1, concat_axis=0, tiled=True)  12.5 us
    split x2, local copies, waits for them, and re-layouts, side_by_side(): jnp.split(result, [sum(widths[:k]) for k in range(1, len(widths))], axis=...  9.03 us
    transpose x1, other arithmetic, body(): joined_block = jnp.transpose(jnp.concatenate(head_block, axis=0))  7.7 us
  transfers between devices with their start and end apart: 5, of which 3 were waited for; matrix products, arithmetic and copies ran while one was open for 16% of the time, Pallas kernels for 0%

commit v1 on v0

--- a/solution.py
+++ b/solution.py
@@ -1,17 +1,227 @@
 import jax
 import jax.numpy as jnp
 from jax import lax
+from jax.experimental import pallas as pl
+from jax.experimental.pallas import tpu as pltpu
 from jax.sharding import PartitionSpec as P
 
 score_scale = 144.0 ** (-0.5)
 soft_cap = 50.0
 
 
-def side_by_side(arrays, axis, dim, along):
-    widths = [a.shape[along] for a in arrays]
-    both = jnp.concatenate(arrays, axis=along)
-    result = lax.all_gather(both, axis, axis=dim, tiled=True)
-    return tuple(jnp.split(result, [sum(widths[:k]) for k in range(1, len(widths))], axis=along))
+MESH = pl.DeviceIdType.MESH
+
+
+def gather_kernel(q_ref, k_ref, v_ref, o_ref, outq_ref, outo_ref, s1q, s1o, so, gq, go,
+                  s1_send, s1_recv, z_send, z_recv, x_send, x_recv, d_send, d_recv, out_sem):
+    rep = lax.axis_index("rep")
+    tp = lax.axis_index("tp")
+    h = rep // 8
+    z = (rep // 2) % 4
+    core = rep % 2
+    g = 2 * h + core
+    gpar = 2 * (1 - h) + core
+    zp = (z + 1) % 4
+    zm = (z + 3) % 4
+    zo = (z + 2) % 4
+    gathered = (gq, go)
+    halves = (gq.shape[2] // 2, go.shape[2] // 2)
+    outs = (outq_ref, outo_ref)
+    piece_z = (z, zm, zp, zo)
+    piece_g = (g, gpar)
+
+    def remote(src, dst, ssem, rsem, device):
+        return pltpu.make_async_remote_copy(
+            src_ref=src, dst_ref=dst, send_sem=ssem, recv_sem=rsem, device_id=device,
+            device_id_type=MESH)
+
+    def exchange(src, dst, dest_rep, dest_tp, ssem, rsem):
+        own = jnp.logical_and(dest_rep == rep, dest_tp == tp)
+
+        @pl.when(own)
+        def _():
+            pltpu.make_async_copy(src, dst, rsem).start()
+
+        @pl.when(jnp.logical_not(own))
+        def _():
+            remote(src, dst, ssem, rsem, (dest_rep, dest_tp)).start()
+
+    def exchange_done(src, dst, dest_rep, dest_tp, ssem, rsem):
+        own = jnp.logical_and(dest_rep == rep, dest_tp == tp)
+
+        @pl.when(jnp.logical_not(own))
+        def _():
+            remote(src, dst, ssem, rsem, (dest_rep, dest_tp)).wait_send()
+
+    block = rep // 2
+    kk = rep % 2
+    width = s1q.shape[1]
+    qrows, krows = q_ref.shape[0], k_ref.shape[0]
+    sends = []
+    for zd in range(4):
+        cols = pl.ds(zd * width, width)
+        sends.append((q_ref.at[:, cols], s1q.at[pl.ds(pl.multiple_of(tp * qrows, qrows), qrows)],
+                      2 * zd + kk, block, s1_send.at[3 * zd], s1_recv.at[0]))
+        row = pl.multiple_of(kk * 128 + tp * krows, krows)
+        sends.append((k_ref.at[:, cols], s1q.at[pl.ds(row, krows)],
+                      8 + 2 * zd, block, s1_send.at[3 * zd + 1], s1_recv.at[0]))
+        sends.append((v_ref.at[:, cols], s1q.at[pl.ds(row, krows)],
+                      9 + 2 * zd, block, s1_send.at[3 * zd + 2], s1_recv.at[0]))
+    zdest = rep // 4
+    slot = (rep % 4) * 8 + tp
+    for p in range(8):
+        for gd in range(4):
+            sends.append((o_ref.at[:, pl.ds(p * 512 + gd * 128, 128)], s1o.at[slot],
+                          (gd // 2) * 8 + zdest * 2 + gd % 2, p,
+                          s1_send.at[12 + 4 * p + gd], s1_recv.at[1]))
+    for item in sends:
+        exchange(*item)
+
+    def chunk(a, zs, gs, half):
+        return gathered[a].at[zs, gs, pl.ds(half * halves[a], halves[a])]
+
+    def out_slice(a, zs, gs, half):
+        if a == 0:
+            rows = pl.ds(pl.multiple_of(zs * 1152 + half * 576, 576), 576)
+            return outs[a].at[rows, pl.ds(pl.multiple_of(gs * 256, 256), 256)]
+        rows = pl.ds(pl.multiple_of(gs * 128 + half * 64, 64), 64)
+        return outs[a].at[rows, pl.ds(pl.multiple_of(zs * 1152, 1152), 1152)]
+
+    def write_out(a, zs, gs, half):
+        pltpu.make_async_copy(chunk(a, zs, gs, half), out_slice(a, zs, gs, half), out_sem.at[a]).start()
+
+    def d2d(a, xp, s):
+        c = chunk(a, piece_z[s // 2], piece_g[xp], s % 2)
+        i = (a * 2 + xp) * 8 + s
+        return remote(c, c, d_send.at[i], d_recv.at[i], (rep + 1 - 2 * core, tp))
+
+    def arrived(a, xp, s):
+        d2d(a, xp, s).start()
+        write_out(a, piece_z[s // 2], piece_g[xp], s % 2)
+
+    def d2d_arrived(a, xp, s):
+        d2d(a, xp, s).wait_recv()
+        write_out(a, piece_z[s // 2], piece_g[xp] + 1 - 2 * core, s % 2)
+
+    up = (h * 8 + zp * 2 + core, tp)
+    down = (h * 8 + zm * 2 + core, tp)
+
+    def zcopy(a, xp, i):
+        zs, half, to = ((z, 0, up), (z, 1, up), (z, 0, down), (z, 1, down), (zm, 0, up), (zp, 1, down))[i]
+        c = chunk(a, zs, piece_g[xp], half)
+        j = (a * 2 + xp) * 6 + i
+        return remote(c, c, z_send.at[j], z_recv.at[j], to)
+
+    def xcopy(a, half):
+        c = chunk(a, z, g, half)
+        return remote(c, c, x_send.at[2 * a + half], x_recv.at[2 * a + half],
+                      ((1 - h) * 8 + z * 2 + core, tp))
+
+    def launch(a, xp):
+        for i in (0, 3, 1, 2):
+            zcopy(a, xp, i).start()
+        arrived(a, xp, 0)
+        arrived(a, xp, 1)
+
+    def relay(a, xp):
+        zcopy(a, xp, 0).wait_recv()
+        zcopy(a, xp, 4).start()
+        arrived(a, xp, 2)
+        zcopy(a, xp, 3).wait_recv()
+        zcopy(a, xp, 5).start()
+        arrived(a, xp, 5)
+        zcopy(a, xp, 1).wait_recv()
+        arrived(a, xp, 3)
+        zcopy(a, xp, 2).wait_recv()
+        arrived(a, xp, 4)
+
+    def finish(a, xp):
+        zcopy(a, xp, 4).wait_recv()
+        arrived(a, xp, 6)
+        zcopy(a, xp, 5).wait_recv()
+        arrived(a, xp, 7)
+
+    pltpu.make_async_copy(s1q, s1q, s1_recv.at[0]).wait()
+    for b in range(9):
+        for c in range(2):
+            tile = s1q[c * 128:(c + 1) * 128, b * 128:(b + 1) * 128].astype(jnp.float32)
+            gq[z, g, b * 128:(b + 1) * 128, c * 128:(c + 1) * 128] = tile.T.astype(jnp.bfloat16)
+    xcopy(0, 0).start()
+    xcopy(0, 1).start()
+    launch(0, 0)
+    pltpu.make_async_copy(s1o, s1o, s1_recv.at[1]).wait()
+    nrow = s1o.shape[1]
+    for i in range(32):
+        so[i * nrow:(i + 1) * nrow, :] = s1o[i].astype(jnp.float32)
+    for b in range(9):
+        go[z, g, :, b * 128:(b + 1) * 128] = so[b * 128:(b + 1) * 128, :].T.astype(jnp.bfloat16)
+    xcopy(1, 0).start()
+    xcopy(1, 1).start()
+    launch(1, 0)
+    relay(0, 0)
+    relay(1, 0)
+    xcopy(0, 0).wait_recv()
+    xcopy(0, 1).wait_recv()
+    launch(0, 1)
+    for s in range(6):
+        d2d_arrived(0, 0, s)
+    finish(0, 0)
+    for s in range(6):
+        d2d_arrived(1, 0, s)
+    finish(1, 0)
+    xcopy(1, 0).wait_recv()
+    xcopy(1, 1).wait_recv()
+    launch(1, 1)
+    for a in range(2):
+        d2d_arrived(a, 0, 6)
+        d2d_arrived(a, 0, 7)
+        d2d_arrived(a, 1, 0)
+        d2d_arrived(a, 1, 1)
+    relay(0, 1)
+    relay(1, 1)
+    for s in range(2, 6):
+        d2d_arrived(0, 1, s)
+    finish(0, 1)
+    for s in range(2, 6):
+        d2d_arrived(1, 1, s)
+    finish(1, 1)
+    for a in range(2):
+        d2d_arrived(a, 1, 6)
+        d2d_arrived(a, 1, 7)
+    for item in sends:
+        exchange_done(*item)
+    for a in range(2):
+        xcopy(a, 0).wait_send()
+        xcopy(a, 1).wait_send()
+        for xp in range(2):
+            for i in range(6):
+                zcopy(a, xp, i).wait_send()
+            for s in range(8):
+                d2d(a, xp, s).wait_send()
+        pltpu.make_async_copy(outs[a], outs[a], out_sem.at[a]).wait()
+
+
+def gather_blocks(q, k, v, o):
+    bf = jnp.bfloat16
+    dma = pltpu.SemaphoreType.DMA
+    return pl.pallas_call(
+        gather_kernel,
+        out_shape=(jax.ShapeDtypeStruct((4608, 1024), bf), jax.ShapeDtypeStruct((512, 4608), bf)),
+        in_specs=[pl.BlockSpec(memory_space=pl.ANY)] * 4,
+        out_specs=[pl.BlockSpec(memory_space=pl.ANY)] * 2,
+        scratch_shapes=[
+            pltpu.VMEM((256, 1152), bf),
+            pltpu.VMEM((32, 36, 128), bf),
+            pltpu.VMEM((1152, 128), jnp.float32),
+            pltpu.VMEM((4, 4, 1152, 256), bf),
+            pltpu.VMEM((4, 4, 128, 1152), bf),
+            dma((44,)), dma((2,)), dma((24,)), dma((24,)), dma((4,)), dma((4,)),
+            dma((32,)), dma((32,)), dma((2,)),
+        ],
+        compiler_params=pltpu.CompilerParams(
+            has_side_effects=True, vmem_limit_bytes=48 * 1024 * 1024),
+        name="gather_blocks",
+    )(q, k, v, o)
 
 
 def sent_to_all(shard, axis):
@@ -46,26 +256,10 @@
 def body(
     hidden, positions, key_cache, value_cache, norm_gain, q_proj, k_proj, v_proj, o_proj, post_gain
 ):
-    tp_count = lax.axis_size("tp")
-    replica_count = lax.axis_size("rep")
-    per_tp = replica_count // tp_count
-    model_width = hidden.shape[1]
-    stacked = side_by_side((q_proj[None], k_proj[None], v_proj[None]), "rep", 0, 1)
-    shaped = [matrix.reshape((tp_count, per_tp, 1) + matrix.shape[1:]) for matrix in stacked]
-    arrived = (
-        lax.all_to_all(shaped[0], "tp", split_axis=0, concat_axis=2, tiled=True),
-        lax.all_to_all(shaped[1], "tp", split_axis=0, concat_axis=2, tiled=True),
-        lax.all_to_all(shaped[2], "tp", split_axis=0, concat_axis=2, tiled=True),
-    )
-    head_block = [matrix.reshape(-1, model_width) for matrix in arrived]
-    joined_block = jnp.transpose(jnp.concatenate(head_block, axis=0))
-    split_cols = o_proj.reshape(o_proj.shape[0], tp_count, -1)
-    rows_of_group = lax.all_to_all(split_cols, "tp", split_axis=1, concat_axis=0, tiled=True)
-    complete_rows = lax.all_gather(rows_of_group, "rep", axis=0, tiled=True)
-    out_block = jnp.transpose(complete_rows.reshape(model_width, -1))
+    joined_block, out_block = gather_blocks(q_proj, k_proj, v_proj, o_proj)
     batch, kv_local, length, head_dim = key_cache.shape
-    q_width = head_block[0].shape[0]
-    kv_width = head_block[1].shape[0]
+    q_width = out_block.shape[0]
+    kv_width = (joined_block.shape[1] - q_width) // 2
     q_local = q_width // head_dim
     group = q_local // kv_local
     normed = rms_scale(hidden.astype(jnp.float32), norm_gain).astype(jnp.bfloat16)

time: 275 us -> 176 us (0.64)
  waiting for transfers between devices: 136 us -> 9.89 us
  Pallas kernels: 0 us -> 109 us
  blocking collectives: 48.2 us -> 0 us
  local copies, waits for them, and re-layouts: 41.4 us -> 18.1 us
  between operations: 14.2 us -> 0.74 us
  starting transfers between devices: 12.7 us -> 22.5 us
  other arithmetic: 11.4 us -> 2.48 us
  matrix products: 9.81 us -> 12.9 us
    pallas_call x0 -> x1, Pallas kernels: none -> 109 us  [gather_blocks(): pl.pallas_call(gather_kernel, out_shape=(jax.ShapeDtypeStruct((4608, 1024...]
    all_gather x2 -> x0, waiting for transfers between devices: 68 us -> none  [the longest x1 68 us: side_by_side(): result = lax.all_gather(both, axis, axis=dim, tiled=True)]
    all_to_all x2 -> x0, waiting for transfers between devices: 67.9 us -> none  [the longest x1 40.9 us: body(): lax.all_to_all(shaped[0], 'tp', split_axis=0, concat_axis=2, tiled=True)]
    all_to_all x2 -> x0, blocking collectives: 48.2 us -> none  [the longest x1 35.7 us: body(): lax.all_to_all(shaped[1], 'tp', split_axis=0, concat_axis=2, tiled=True)]
    all_to_all x1, starting transfers between devices: 3.55 us -> 22.5 us  [sent_to_all(): lax.all_to_all(jnp.broadcast_to(shard[None], (size, *shard.shape)), axis,...]
    all_to_all x4 -> x0, local copies, waits for them, and re-layouts: 10.1 us -> none  [the longest x1 3.23 us: body(): lax.all_to_all(shaped[1], 'tp', split_axis=0, concat_axis=2, tiled=True)]
    all_to_all x1, waiting for transfers between devices: 0.01 us -> 9.89 us  [sent_to_all(): lax.all_to_all(jnp.broadcast_to(shard[None], (size, *shard.shape)), axis,...]
    all_to_all x2 -> x0, starting transfers between devices: 9.11 us -> none  [the longest x1 4.74 us: body(): lax.all_to_all(shaped[0], 'tp', split_axis=0, concat_axis=2, tiled=True)]
  transfers between devices with their start and end apart: 5 -> 1, of which waited for: 3 -> 1; matrix products, arithmetic and copies ran while one was open for 16% -> 0% of each run, Pallas kernels for 0% -> 0%
where the time goes in v1:
time: 176 us; the launch traced here: 175 us
  Pallas kernels  109 us (62%)
  starting transfers between devices  22.5 us (13%)
  local copies, waits for them, and re-layouts  18.1 us (10%)
  matrix products  12.9 us (7%)
  waiting for transfers between devices  9.89 us (6%)
  other arithmetic  2.48 us (1%)
    pallas_call x1, Pallas kernels, gather_blocks(): pl.pallas_call(gather_kernel, out_shape=(jax.ShapeDtypeStruct((4608, 1024...  109 us
    all_to_all x1, starting transfers between devices, sent_to_all(): lax.all_to_all(jnp.broadcast_to(shard[None], (size, *shard.shape)), axis,...  22.5 us
    unnamed x18, local copies, waits for them, and re-layouts  17.1 us
    all_to_all x1, waiting for transfers between devices, sent_to_all(): lax.all_to_all(jnp.broadcast_to(shard[None], (size, *shard.shape)), axis,...  9.89 us
    dot_general x1, matrix products, body(): jnp.dot(normed, joined_block, preferred_element_type=jnp.float32)  6.79 us
  transfers between devices with their start and end apart: 1, of which 1 were waited for; matrix products, arithmetic and copies ran while one was open for 0% of the time, Pallas kernels for 0%

profile of v1, /device:TPU:1, one launch (start us, length us, event | category | flops | bytes accessed | tf_op | source)
XLA Modules:
  0.0 175.2 jit_solution(16594870468217679008)
XLA Ops:
  0.7 1.1 fusion.5
  1.7 1.0 copy-done.2
  2.7 1.0 copy-done.3
  3.7 0.9 copy-done.4
  4.6 0.9 copy-done.5
  5.5 108.6 %gather_blocks.1 = (bf16[4608,1024]{1,0:T(8,128)(2,1)}, bf16[512,4608]{1,0:T(8,128)(2,1)S(1)}) custom-call(bf16[32,4608]{1,0:T(8,128)(2,1)S(1)} %copy-done.3, bf16[16,4608]{1,0:T(8,128)(2,1)S(1)} %copy-done.4, bf16[16,4608]{1,0:T(8,128)(2,1)S(1)} %copy-done.5, bf16[36,4096]{1,0:T(8,128)(2,1)S(1)} %copy-done.2), custom_call_target="tpu_custom_call" | custom-call | tf_op jit(solution)/shard_map/gather_blocks/pallas_call | solution.py:207
  114.1 6.8 %fusion.8 = f32[4,1024]{1,0:T(4,128)S(1)} fusion(bf16[4608,1024]{1,0:T(8,128)(2,1)} %get-tuple-element.20, bf16[4,4608]{1,0:T(4,128)(2,1)} %param.10, f32[4608]{0:T(1024)} %param.14, f32[4]{0:T(128)S(1)} %add_rsqrt_fusion.1), kind=kOutput, calls=%fused_computation.14 | convolution fusion | flops 37822464 | bytes 9508880 | tf_op jit(solution)/shard_map/dot_general | solution.py:266
  121.0 0.1 iota_compare_fusion
  121.1 0.1 multiply_cosine_fusion
  121.2 0.1 subtract_convert_fusion.1
  121.3 0.1 subtract_convert_fusion
  121.3 0.1 maximum_bitcast_fusion
  121.4 0.2 fusion.13
  121.6 0.8 fusion.18
  122.5 2.0 %fusion.4 = bf16[4,2,2,128]{3,2,1,0:T(2,128)(2,1)S(1)} fusion(bf16[4,2,1024,128]{3,2,1,0:T(8,128)(2,1)} %param.13, f32[4,2,2,1024]{3,2,1,0:T(2,128)S(1)} %get-tuple-element.16, f32[4,2,2]{2,1,0:T(2,128)S(1)} %get-tuple-element.10, f32[4,2,128]{2,1,0:T(2,128)S(1)} %reshape.116, f32[4,2,2]{2,1,0:T(2,128)S(1)} %get-tuple-element.9), kind=kOutput, calls=%fused_computation.6 | convolution fusion | flops 4233216 | bytes 2171008 | tf_op jit(solution)/shard_map/bkgl,bkld->bkgd/dot_general | solution.py:293
  124.5 3.1 %fusion.19 = f32[4,4608]{1,0:T(4,128)S(1)} fusion(bf16[4,512]{1,0:T(4,128)(2,1)S(1)} %convert_element_type.56, bf16[512,4608]{1,0:T(8,128)(2,1)} %copy-done.1), kind=kOutput, calls=%fused_computation.40 | convolution fusion | flops 18874368 | bytes 4796416 | tf_op jit(solution)/shard_map/dot_general | solution.py:301
  127.6 0.9 broadcast_in_dim.12
  128.5 22.5 %all-to-all-start = ((f32[8,4,4608]{2,1,0:T(4,128)}), f32[8,4,4608]{2,1,0:T(4,128)S(1)}, u32[]{:S(2)}, u32[]{:S(2)}) async-start(f32[8,4,4608]{2,1,0:T(4,128)} %broadcast_in_dim.12), calls=%async_computation | async-start | bytes 1179648 | tf_op jit(solution)/shard_map/all_to_all | solution.py:229
  151.0 9.9 %all-to-all-done = f32[8,4,4608]{2,1,0:T(4,128)S(1)} async-done(((f32[8,4,4608]{2,1,0:T(4,128)}), f32[8,4,4608]{2,1,0:T(4,128)S(1)}, u32[]{:S(2)}, u32[]{:S(2)}) %all-to-all-start) | async-done | bytes 589856 | tf_op jit(solution)/shard_map/all_to_all | solution.py:229
  160.8 0.1 reduce_sum.38
  160.9 0.2 multiply_reduce_fusion
  161.1 0.7 multiply_convert_fusion
  161.8 8.5 %copy.21 = bf16[4608,1024]{1,0:T(8,128)(2,1)} copy(bf16[4608,1024]{1,0:T(8,128)(2,1)} %get-tuple-element.20) | data formatting | bytes 18874368
  170.3 4.8 %copy.22 = bf16[512,4608]{1,0:T(8,128)(2,1)} copy(bf16[512,4608]{1,0:T(8,128)(2,1)} %copy-done.1) | data formatting | bytes 9437184
  (24 shorter events, 0.2 us)
Async XLA Ops:
  0.6 121.0 %copy-start = (bf16[4,2,1024,128]{3,2,1,0:T(8,128)(2,1)S(1)}, bf16[4,2,1024,128]{3,2,1,0:T(8,128)(2,1)}, u32[]{:S(2)}) copy-start(bf16[4,2,1024,128]{3,2,1,0:T(8,128)(2,1)} %param.12) | copy-start | bytes 6291460
  1.7 1.0 copy-start.2
  2.7 1.0 copy-start.3
  3.7 0.9 copy-start.4
  4.6 0.9 copy-start.5
  114.1 6.8 %copy-start.1 = (bf16[512,4608]{1,0:T(8,128)(2,1)}, bf16[512,4608]{1,0:T(8,128)(2,1)S(1)}, u32[]{:S(2)}) copy-start(bf16[512,4608]{1,0:T(8,128)(2,1)S(1)} %get-tuple-element.21) | copy-start | bytes 14155780
  114.1 6.8 %copy-start.7 = (s32[4]{0:T(128)S(1)}, s32[4]{0:T(128)}, u32[]{:S(2)}) copy-start(s32[4]{0:T(128)} %param.11) | copy-start | bytes 52
  122.5 38.7 %copy-start.6 = (f32[576]{0:T(1024)S(1)}, f32[576]{0:T(1024)}, u32[]{:S(2)}) copy-start(f32[576]{0:T(1024)} %param.19) | copy-start | bytes 6916
  128.5 32.4 %all-to-all-start = ((f32[8,4,4608]{2,1,0:T(4,128)}), f32[8,4,4608]{2,1,0:T(4,128)S(1)}, u32[]{:S(2)}, u32[]{:S(2)}) async-start(f32[8,4,4608]{2,1,0:T(4,128)} %broadcast_in_dim.12), calls=%async_computation | async-start | bytes 1179648 | tf_op jit(solution)/shard_map/all_to_all | solution.py:229

commit v2 on v1

v2 whole, which is shorter than its diff:
```python
import jax
import jax.numpy as jnp
import numpy as np
from jax import lax
from jax.experimental import pallas as pl
from jax.experimental.pallas import tpu as pltpu
from jax.sharding import PartitionSpec as P

score_scale = 144.0 ** (-0.5)
soft_cap = 50.0
MESH = pl.DeviceIdType.MESH


def remote(src, dst, ssem, rsem, device):
    return pltpu.make_async_remote_copy(
        src_ref=src, dst_ref=dst, send_sem=ssem, recv_sem=rsem, device_id=device,
        device_id_type=MESH)


def gather_kernel(q_ref, k_ref, v_ref, o_ref, gq, go, s1a, s1q, s1o, so,
                  a_send, a_recv, b_send, q_recv, o_send, o_recv, z_send, z_recv, x_send, x_recv,
                  d_send, d_recv):
    rep = lax.axis_index("rep")
    tp = lax.axis_index("tp")
    h = rep // 8
    z = (rep // 2) % 4
    core = rep % 2
    lo = tp // 4
    g = 2 * h + core
    gpar = 2 * (1 - h) + core
    zp = (z + 1) % 4
    zm = (z + 3) % 4
    zo = (z + 2) % 4
    gathered = (gq, go)
    halves = (gq.shape[2] // 2, go.shape[2] // 2)
    piece_z = (z, zm, zp, zo)
    piece_g = (g, gpar)

    def place(h_, z_, c_):
        return h_ * 8 + z_ * 2 + c_

    width = s1q.shape[1]
    qrows, krows = q_ref.shape[0], k_ref.shape[0]
    parts = ((q_ref, 0, qrows), (k_ref, qrows, krows), (v_ref, qrows + krows, krows))

    def along_z(dist, part):
        zd = (z + dist) % 4
        ref, row, rows = parts[part]
        src = ref.at[:, pl.ds(pl.multiple_of(zd * width, width), width)]
        dst = s1a.at[z, pl.ds(row, rows)]
        if dist == 0:
            return pltpu.make_async_copy(src, dst, a_recv.at[0])
        return remote(src, dst, a_send.at[3 * dist + part], a_recv.at[dist], (place(h, zd, core), tp))

    for dist in (2, 1, 3, 0):
        for part in range(3):
            along_z(dist, part).start()

    zdest = rep // 4
    slot = (rep % 4) * 8 + tp

    def o_slice(p, gd):
        src = o_ref.at[:, pl.ds(p * 512 + gd * 128, 128)]
        return src, s1o.at[slot], place(gd // 2, zdest, gd % 2), p, o_send.at[4 * p + gd], o_recv

    def exchange(src, dst, dest_rep, dest_tp, ssem, rsem):
        own = jnp.logical_and(dest_rep == rep, dest_tp == tp)

        @pl.when(own)
        def _():
            pltpu.make_async_copy(src, dst, rsem).start()

        @pl.when(jnp.logical_not(own))
        def _():
            remote(src, dst, ssem, rsem, (dest_rep, dest_tp)).start()

    def exchange_done(src, dst, dest_rep, dest_tp, ssem, rsem):
        own = jnp.logical_and(dest_rep == rep, dest_tp == tp)

        @pl.when(jnp.logical_not(own))
        def _():
            remote(src, dst, ssem, rsem, (dest_rep, dest_tp)).wait_send()

    for p in range(8):
        for gd in range(4):
            exchange(*o_slice(p, gd))

    def to_owner(dist, part):
        zs = (z + dist) % 4
        _, row, rows = parts[part]
        src = s1a.at[zs, pl.ds(row, rows)]
        if part == 0:
            dest, first = place(0, z, core), tp * rows
        else:
            dest, first = place(1, z, part - 1), core * 128 + tp * rows
        dst = s1q.at[pl.ds(pl.multiple_of(first, rows), rows)]
        return src, dst, dest, h * 4 + zs, b_send.at[3 * dist + part], q_recv

    for dist in (0, 1, 3, 2):
        came = s1a.at[(z + dist) % 4]
        pltpu.make_async_copy(came, came, a_recv.at[(4 - dist) % 4]).wait()
        for part in range(3):
            exchange(*to_owner(dist, part))

    def chunk(a, zs, gs, half):
        return gathered[a].at[zs, gs, pl.ds(half * halves[a], halves[a])]

    def d2d(a, xp, s):
        c = chunk(a, piece_z[s // 2], piece_g[xp], s % 2)
        i = (a * 2 + xp) * 8 + s
        return remote(c, c, d_send.at[i], d_recv.at[i], (place(h, z, 1 - core), tp))

    up = (place(h, zp, core), tp)
    down = (place(h, zm, core), tp)

    def zcopy(a, xp, i):
        zs, half, to = ((z, 0, up), (z, 1, up), (z, 0, down), (z, 1, down), (zm, 0, up), (zp, 1, down))[i]
        c = chunk(a, zs, piece_g[xp], half)
        j = (a * 2 + xp) * 6 + i
        return remote(c, c, z_send.at[j], z_recv.at[j], to)

    def xcopy(a, s):
        c = chunk(a, piece_z[s // 2], g, s % 2)
        return remote(c, c, x_send.at[a * 8 + s], x_recv.at[a * 8 + s], (place(1 - h, z, core), tp))

    def arrived(a, xp, s):
        if a == 1:
            xcopy(1, s).start()
        d2d(a, xp, s).start()

    def launch(a, xp):
        for i in (0, 3, 1, 2):
            zcopy(a, xp, i).start()
        arrived(a, xp, 0)
        arrived(a, xp, 1)

    def relay(a, xp):
        zcopy(a, xp, 0).wait_recv()
        zcopy(a, xp, 4).start()
        arrived(a, xp, 2)
        zcopy(a, xp, 3).wait_recv()
        zcopy(a, xp, 5).start()
        arrived(a, xp, 5)
        zcopy(a, xp, 1).wait_recv()
        arrived(a, xp, 3)
        zcopy(a, xp, 2).wait_recv()
        arrived(a, xp, 4)

    def finish(a, xp):
        zcopy(a, xp, 4).wait_recv()
        arrived(a, xp, 6)
        zcopy(a, xp, 5).wait_recv()
        arrived(a, xp, 7)

    pltpu.make_async_copy(s1o, s1o, o_recv).wait()
    nrow = s1o.shape[1]
    for i in range(32):
        so[i * nrow:(i + 1) * nrow, :] = s1o[i].astype(jnp.float32)
    for b in range(9):
        go[z, g, :, b * 128:(b + 1) * 128] = so[b * 128:(b + 1) * 128, :].T.astype(jnp.bfloat16)
    launch(1, 0)
    pltpu.make_async_copy(s1q, s1q, q_recv).wait()
    for b in range(9):
        for c in range(2):
            tile = s1q[c * 128:(c + 1) * 128, b * 128:(b + 1) * 128].astype(jnp.float32)
            gq[z, g, b * 128:(b + 1) * 128, c * 128:(c + 1) * 128] = tile.T.astype(jnp.bfloat16)
    xcopy(0, 0).start()
    xcopy(0, 1).start()
    launch(0, 0)
    relay(1, 0)
    finish(1, 0)
    relay(0, 0)
    for s in range(2):
        xcopy(0, s).wait_recv()
    launch(0, 1)
    finish(0, 0)
    for s in range(8):
        xcopy(1, s).wait_recv()
        d2d(1, 1, s).start()
    relay(0, 1)
    finish(0, 1)
    for a, xp in ((1, 0), (0, 0), (1, 1), (0, 1)):
        for s in range(8):
            d2d(a, xp, s).wait_recv()
    for part in range(3):
        for dist in (1, 2, 3):
            along_z(dist, part).wait_send()
        for dist in range(4):
            exchange_done(*to_owner(dist, part))
    for p in range(8):
        for gd in range(4):
            exchange_done(*o_slice(p, gd))
    for s in range(2):
        xcopy(0, s).wait_send()
    for s in range(8):
        xcopy(1, s).wait_send()
    for a, xp in ((1, 0), (0, 0), (1, 1), (0, 1)):
        if (a, xp) != (1, 1):
            for i in range(6):
                zcopy(a, xp, i).wait_send()
        for s in range(8):
            d2d(a, xp, s).wait_send()


def gather_blocks(q, k, v, o):
    bf = jnp.bfloat16
    dma = pltpu.SemaphoreType.DMA
    return pl.pallas_call(
        gather_kernel,
        out_shape=(jax.ShapeDtypeStruct((4, 4, 1152, 256), bf),
                   jax.ShapeDtypeStruct((4, 4, 128, 1152), bf)),
        in_specs=[pl.BlockSpec(memory_space=pltpu.HBM)] * 4,
        out_specs=[pl.BlockSpec(memory_space=pltpu.VMEM)] * 2,
        scratch_shapes=[
            pltpu.VMEM((4, 64, 1152), bf),
            pltpu.VMEM((256, 1152), bf),
            pltpu.VMEM((32, 36, 128), bf),
            pltpu.VMEM((1152, 128), jnp.float32),
            dma((12,)), dma((4,)), dma((12,)), dma, dma((32,)), dma,
            dma((24,)), dma((24,)), dma((16,)), dma((16,)), dma((32,)), dma((32,)),
        ],
        compiler_params=pltpu.CompilerParams(
            has_side_effects=True, vmem_limit_bytes=8 * 1024 * 1024),
        name="gather_blocks",
    )(q, k, v, o)


def attend_kernel(pos_ref, gq, go, hidden_ref, gain_ref, freq_ref, kc, vc, joined_ref, wo_ref, part_ref,
                  out_sem):
    copies = []
    for zs in range(4):
        for gs in range(4):
            copies.append((gq.at[zs, gs], joined_ref.at[pl.ds(zs * 1152, 1152), pl.ds(gs * 256, 256)], 0))
            copies.append((go.at[zs, gs], wo_ref.at[pl.ds(gs * 128, 128), pl.ds(zs * 1152, 1152)], 1))
    for src, dst, i in copies:
        pltpu.make_async_copy(src, dst, out_sem.at[i]).start()
    f32, bf = jnp.float32, jnp.bfloat16
    hid = hidden_ref[...].astype(f32)
    mean_square = jnp.mean(hid * hid, axis=-1, keepdims=True)
    normed = (hid * lax.rsqrt(mean_square + 1e-06) * gain_ref[...]).astype(bf)
    proj = []
    for gs in range(4):
        acc = jnp.zeros((4, 256), f32)
        for zs in range(4):
            acc += jnp.dot(normed[:, zs * 1152:(zs + 1) * 1152], gq[zs, gs], preferred_element_type=f32)
        proj += [acc[:, :128], acc[:, 128:]]
    row = lax.broadcasted_iota(jnp.int32, (4, 128), 0)
    posf = jnp.zeros((4, 128), f32)
    for b in range(4):
        posf = jnp.where(row == b, pos_ref[b].astype(f32), posf)
    angle = posf * freq_ref[...]
    lane = lax.broadcasted_iota(jnp.int32, (4, 128), 1)
    cosine = jnp.cos(angle)
    sine = jnp.where(lane < 64, -jnp.sin(angle), jnp.sin(angle))

    def rotate(x):
        swapped = jnp.concatenate([x[:, 64:], x[:, :64]], axis=1)
        return (x * cosine + swapped * sine).astype(bf).astype(f32)

    query = jnp.concatenate([rotate(x) for x in proj[:4]], axis=0)
    keys = [rotate(x) for x in proj[4:6]]
    vals = [x.astype(bf).astype(f32) for x in proj[6:8]]
    keys_new = jnp.concatenate([keys[0], keys[0], keys[1], keys[1]], axis=0)
    values_new = jnp.concatenate([vals[0], vals[0], vals[1], vals[1]], axis=0)
    qb = query.astype(bf)
    length = kc.shape[2]
    r = lax.broadcasted_iota(jnp.int32, (16, length), 0)
    slot = lax.broadcasted_iota(jnp.int32, (16, length), 1)
    owner = (r // 8) * 4 + r % 4
    scores = jnp.zeros((16, length), f32)
    limit = jnp.zeros((16, length), jnp.int32)
    for kv in range(2):
        for b in range(4):
            s = lax.dot_general(qb, kc[b, kv], (((1,), (1,)), ((), ())), preferred_element_type=f32)
            scores = jnp.where(owner == kv * 4 + b, s, scores)
    for b in range(4):
        limit = jnp.where(r % 4 == b, pos_ref[b], limit)
    capped = soft_cap * jnp.tanh(scores * score_scale / soft_cap)
    raw = jnp.where(slot < limit, jnp.exp(capped), 0.0)
    self_score = jnp.sum(query * keys_new, axis=-1, keepdims=True) * score_scale
    self_raw = jnp.exp(soft_cap * jnp.tanh(self_score / soft_cap))
    denom = jnp.sum(raw, axis=-1, keepdims=True) + self_raw
    weights = (raw / denom).astype(bf).astype(f32)
    attention = (self_raw / denom).astype(bf).astype(f32) * values_new
    for kv in range(2):
        for b in range(4):
            w = jnp.where(owner == kv * 4 + b, weights, 0.0).astype(bf)
            attention += jnp.dot(w, vc[b, kv], preferred_element_type=f32)
    att = jnp.concatenate([attention[i * 4:(i + 1) * 4] for i in range(4)], axis=1).astype(bf)
    for zs in range(4):
        part = jnp.dot(att, go[zs].reshape(512, 1152), preferred_element_type=f32)
        part_ref[2 * zs] = part[:, :576]
        part_ref[2 * zs + 1] = part[:, 576:]
    pltpu.make_async_copy(joined_ref, joined_ref, out_sem.at[0]).wait()
    pltpu.make_async_copy(wo_ref, wo_ref, out_sem.at[1]).wait()


def attend(positions, gq, go, hidden, norm_gain, key_cache, value_cache):
    bf = jnp.bfloat16
    vmem = pl.BlockSpec(memory_space=pltpu.VMEM)
    hbm = pl.BlockSpec(memory_space=pltpu.HBM)
    freq = 10000.0 ** (-2.0 * np.arange(64, dtype=np.float64) / 128)
    freq = np.concatenate([freq, freq]).astype(np.float32)[None]
    return pl.pallas_call(
        attend_kernel,
        out_shape=(jax.ShapeDtypeStruct((4608, 1024), bf), jax.ShapeDtypeStruct((512, 4608), bf),
                   jax.ShapeDtypeStruct((8, 4, 576), jnp.float32)),
        in_specs=[pl.BlockSpec(memory_space=pltpu.SMEM)] + [vmem] * 7,
        out_specs=[hbm, hbm, vmem],
        scratch_shapes=[pltpu.SemaphoreType.DMA((2,))],
        compiler_params=pltpu.CompilerParams(vmem_limit_bytes=20 * 1024 * 1024),
        name="attend",
    )(positions, gq, go, hidden, norm_gain.reshape(1, -1), jnp.asarray(freq), key_cache, value_cache)


def norm_kernel(part_ref, gain_ref, out_ref, came, square, squares, p_send, p_recv, s_send, s_recv):
    rep = lax.axis_index("rep")
    tp = lax.axis_index("tp")
    barrier = pltpu.get_barrier_semaphore()
    for d in range(1, 8):
        pl.semaphore_signal(barrier, inc=1, device_id=(rep, (tp + d) % 8), device_id_type=MESH)
    pl.semaphore_wait(barrier, 7)

    def part(d):
        to = (tp + d) % 8
        return remote(part_ref.at[to], came.at[d - 1], p_send.at[d - 1], p_recv.at[d - 1], (rep, to))

    def sq(d):
        return remote(square, squares.at[d - 1], s_send.at[d - 1], s_recv.at[d - 1],
                      (rep, (tp + d) % 8))

    for d in range(1, 8):
        part(d).start()
    total = part_ref[tp]
    for d in range(1, 8):
        part(d).wait_recv()
        total += came[d - 1]
    square[...] = jnp.broadcast_to(jnp.sum(total * total, axis=-1, keepdims=True), square.shape)
    for d in range(1, 8):
        sq(d).start()
    whole = square[...]
    for d in range(1, 8):
        sq(d).wait_recv()
        whole += squares[d - 1]
    scale = lax.rsqrt(whole[:, :1] / 4608.0 + 1e-06)
    out_ref[...] = (total * scale * gain_ref[...]).astype(jnp.bfloat16)
    for d in range(1, 8):
        part(d).wait_send()
        sq(d).wait_send()


def norm_sums(part, post_gain):
    vmem = pl.BlockSpec(memory_space=pltpu.VMEM)
    dma = pltpu.SemaphoreType.DMA
    return pl.pallas_call(
        norm_kernel,
        out_shape=jax.ShapeDtypeStruct((4, 576), jnp.bfloat16),
        in_specs=[vmem, vmem],
        out_specs=vmem,
        scratch_shapes=[pltpu.VMEM((7, 4, 576), jnp.float32), pltpu.VMEM((4, 128), jnp.float32),
                        pltpu.VMEM((7, 4, 128), jnp.float32), dma((7,)), dma((7,)), dma((7,)), dma((7,))],
        compiler_params=pltpu.CompilerParams(has_side_effects=True, collective_id=1),
        name="norm_sums",
    )(part, post_gain.reshape(1, -1))


def body(
    hidden, positions, key_cache, value_cache, norm_gain, q_proj, k_proj, v_proj, o_proj, post_gain
):
    gq, go = gather_blocks(q_proj, k_proj, v_proj, o_proj)
    joined, wo, part = attend(positions, gq, go, hidden, norm_gain, key_cache, value_cache)
    return joined, wo, norm_sums(part, post_gain)


def solution(mesh):
    in_specs = (
        P("rep", None),
        P("rep"),
        P("rep", "tp", None, None),
        P("rep", "tp", None, None),
        P(),
        P(("rep", "tp"), None),
        P(("rep", "tp"), None),
        P(("rep", "tp"), None),
        P(("rep", "tp"), None),
        P("tp"),
    )
    out_specs = (P(None, "tp"), P("tp", None), P("rep", "tp"))
    return jax.shard_map(body, mesh=mesh, in_specs=in_specs, out_specs=out_specs, check_vma=False)
```

time: 176 us -> 159 us (0.903)
  Pallas kernels: 109 us -> 144 us
  starting transfers between devices: 22.5 us -> 0 us
  matrix products: 12.9 us -> 0 us
  waiting for transfers between devices: 9.89 us -> 0 us
  local copies, waits for them, and re-layouts: 18.1 us -> 12.2 us
  other arithmetic: 2.48 us -> 0 us
    pallas_call x1 -> x3, Pallas kernels: 109 us -> 144 us  [the longest x1 124 us: gather_blocks(): pl.pallas_call(gather_kernel, out_shape=(jax.ShapeDtypeStruct((4, 4, 1152...]
    all_to_all x1 -> x0, starting transfers between devices: 22.5 us -> none  [sent_to_all(): lax.all_to_all(jnp.broadcast_to(shard[None], (size, *shard.shape)), axis,...]
    dot_general x5 -> x0, matrix products: 12.9 us -> none  [the longest x1 6.79 us: body(): jnp.dot(normed, joined_block, preferred_element_type=jnp.float32)]
    all_to_all x1 -> x0, waiting for transfers between devices: 9.89 us -> none  [sent_to_all(): lax.all_to_all(jnp.broadcast_to(shard[None], (size, *shard.shape)), axis,...]
    unnamed x18 -> x23, local copies, waits for them, and re-layouts: 17.1 us -> 10.9 us
  transfers between devices with their start and end apart: 1 -> 0, of which waited for: 1 -> 0; matrix products, arithmetic and copies ran while one was open for 0% -> 0% of each run, Pallas kernels for 0% -> 0%
where the time goes in v2:
time: 159 us; the launch traced here: 157 us
  Pallas kernels  144 us (91%)
  local copies, waits for them, and re-layouts  12.2 us (8%)
    pallas_call x1, Pallas kernels, gather_blocks(): pl.pallas_call(gather_kernel, out_shape=(jax.ShapeDtypeStruct((4, 4, 1152...  124 us
    pallas_call x1, Pallas kernels, norm_sums(): pl.pallas_call(norm_kernel, out_shape=jax.ShapeDtypeStruct((4, 576), jnp....  12 us
    unnamed x23, local copies, waits for them, and re-layouts  10.9 us
    pallas_call x1, Pallas kernels, attend(): pl.pallas_call(attend_kernel, out_shape=(jax.ShapeDtypeStruct((4608, 1024...  7.42 us

profile of v2, /device:TPU:1, one launch (start us, length us, event | category | flops | bytes accessed | tf_op | source)
XLA Modules:
  0.0 156.9 jit_solution(8145284353283660693)
XLA Ops:
  0.6 0.0 copy-start.2
  0.6 1.0 copy-done.2
  1.6 0.0 copy-start.3
  1.6 1.0 copy-done.3
  2.6 0.0 copy-start.4
  2.6 0.9 copy-done.4
  3.5 0.0 copy-start.5
  3.5 0.9 copy-done.5
  4.4 124.5 %gather_blocks.1 = (bf16[4,4,1152,256]{3,2,1,0:T(8,128)(2,1)S(1)}, bf16[4,4,128,1152]{3,2,1,0:T(8,128)(2,1)S(1)}) custom-call(bf16[32,4608]{1,0:T(8,128)(2,1)S(1)} %copy-done.3, bf16[16,4608]{1,0:T(8,128)(2,1)S(1)} %copy-done.4, bf16[16,4608]{1,0:T(8,128)(2,1)S(1)} %copy-done.5, bf16[36,4096]{1,0:T(8,128)(2,1)S(1)} %copy-done.2), custom_call_target="tpu_custom_call" | custom-call | tf_op jit(solution)/shard_map/gather_blocks/pallas_call | solution.py:208
  128.9 0.7 reshape.12.gain_ref
  129.6 0.0 copy-start
  129.6 1.6 %copy-done = bf16[4,2,1024,128]{3,2,1,0:T(8,128)(2,1)S(1)} copy-done((bf16[4,2,1024,128]{3,2,1,0:T(8,128)(2,1)S(1)}, bf16[4,2,1024,128]{3,2,1,0:T(8,128)(2,1)}, u32[]{:S(2)}) %copy-start) | copy-done | bytes 2097176
  131.2 0.0 copy-start.1
  131.2 1.6 %copy-done.1 = bf16[4,2,1024,128]{3,2,1,0:T(8,128)(2,1)S(1)} copy-done((bf16[4,2,1024,128]{3,2,1,0:T(8,128)(2,1)S(1)}, bf16[4,2,1024,128]{3,2,1,0:T(8,128)(2,1)}, u32[]{:S(2)}) %copy-start.1) | copy-done | bytes 2097176
  132.8 0.8 copy-done.7
  133.6 0.7 copy-done.8
  134.2 0.7 copy-done.9
  134.9 7.4 %attend.1 = (bf16[4608,1024]{1,0:T(8,128)(2,1)}, bf16[512,4608]{1,0:T(8,128)(2,1)}, f32[8,4,576]{2,1,0:T(4,128)S(1)}) custom-call(s32[4]{0:T(128)S(1)} %copy-done.8, bf16[4,4,1152,256]{3,2,1,0:T(8,128)(2,1)S(1)} %get-tuple-element.8.gq, bf16[4,4,128,1152]{3,2,1,0:T(8,128)(2,1)S(1)} %get-tuple-element.9.go, bf16[4,4608]{1,0:T(4,128)(2,1)S(1)} %copy-done.7, ...), custom_call_target="tpu_custom_call" | custom-call | tf_op jit(solution)/shard_map/attend/pallas_call | solution.py:304
  142.3 0.0 copy-start.6
  142.3 0.6 copy-done.6
  142.9 0.0 copy-done.10
  142.9 0.6 reshape.13.gain_ref
  143.5 12.0 %norm_sums.1 = bf16[4,576]{1,0:T(4,128)(2,1)} custom-call(f32[8,4,576]{2,1,0:T(4,128)} %copy-done.6, f32[1,576]{1,0:T(1,128)} %reshape.13.gain_ref), custom_call_target="tpu_custom_call" | custom-call | tf_op jit(solution)/shard_map/norm_sums/pallas_call | solution.py:355
  155.6 1.3 copy.15
  (4 shorter events, 0.0 us)
Async XLA Ops:
  0.6 1.0 copy-start.2
  1.6 1.0 copy-start.3
  2.6 0.9 copy-start.4
  3.5 0.9 copy-start.5
  129.6 1.6 %copy-start = (bf16[4,2,1024,128]{3,2,1,0:T(8,128)(2,1)S(1)}, bf16[4,2,1024,128]{3,2,1,0:T(8,128)(2,1)}, u32[]{:S(2)}) copy-start(bf16[4,2,1024,128]{3,2,1,0:T(8,128)(2,1)} %kc.1) | copy-start | bytes 6291460
  131.2 1.6 %copy-start.1 = (bf16[4,2,1024,128]{3,2,1,0:T(8,128)(2,1)S(1)}, bf16[4,2,1024,128]{3,2,1,0:T(8,128)(2,1)}, u32[]{:S(2)}) copy-start(bf16[4,2,1024,128]{3,2,1,0:T(8,128)(2,1)} %vc.1) | copy-start | bytes 6291460
  132.8 0.8 copy-start.7
  133.6 0.7 copy-start.8
  134.2 0.7 copy-start.9
  134.9 8.1 %copy-start.10 = (f32[576]{0:T(1024)S(1)}, f32[576]{0:T(1024)}, u32[]{:S(2)}) copy-start(f32[576]{0:T(1024)} %param.20) | copy-start | bytes 6916
  142.3 0.6 copy-start.6

commit v3 on v2

--- a/solution.py
+++ b/solution.py
@@ -17,9 +17,10 @@
         device_id_type=MESH)
 
 
-def gather_kernel(q_ref, k_ref, v_ref, o_ref, gq, go, s1a, s1q, s1o, so,
+def gather_kernel(q_ref, k_ref, v_ref, o_ref, hidden_ref, gain_ref, kc_ref, vc_ref,
+                  gq, go, hidden_out, gain_out, kc_out, vc_out, s1a, s1q, s1o, so,
                   a_send, a_recv, b_send, q_recv, o_send, o_recv, z_send, z_recv, x_send, x_recv,
-                  d_send, d_recv):
+                  d_send, d_recv, plane_sem, in_sem):
     rep = lax.axis_index("rep")
     tp = lax.axis_index("tp")
     h = rep // 8
@@ -28,6 +29,7 @@
     lo = tp // 4
     g = 2 * h + core
     gpar = 2 * (1 - h) + core
+    rep_in_plane = g
     zp = (z + 1) % 4
     zm = (z + 3) % 4
     zo = (z + 2) % 4
@@ -55,6 +57,11 @@
     for dist in (2, 1, 3, 0):
         for part in range(3):
             along_z(dist, part).start()
+
+    local = [pltpu.make_async_copy(src, dst, in_sem.at[i]) for i, (src, dst) in enumerate(
+        ((hidden_ref, hidden_out), (gain_ref, gain_out), (kc_ref, kc_out), (vc_ref, vc_out)))]
+    for copy in local:
+        copy.start()
 
     zdest = rep // 4
     slot = (rep % 4) * 8 + tp
@@ -124,8 +131,6 @@
         return remote(c, c, x_send.at[a * 8 + s], x_recv.at[a * 8 + s], (place(1 - h, z, core), tp))
 
     def arrived(a, xp, s):
-        if a == 1:
-            xcopy(1, s).start()
         d2d(a, xp, s).start()
 
     def launch(a, xp):
@@ -160,28 +165,39 @@
         go[z, g, :, b * 128:(b + 1) * 128] = so[b * 128:(b + 1) * 128, :].T.astype(jnp.bfloat16)
     launch(1, 0)
     pltpu.make_async_copy(s1q, s1q, q_recv).wait()
+    for i in range(1, 32):
+        peer = (rep_in_plane + i // 8) % 4
+        pl.semaphore_signal(plane_sem, inc=1, device_id=(place(peer // 2, z, peer % 2), (tp + i) % 8),
+                            device_id_type=MESH)
     for b in range(9):
         for c in range(2):
             tile = s1q[c * 128:(c + 1) * 128, b * 128:(b + 1) * 128].astype(jnp.float32)
             gq[z, g, b * 128:(b + 1) * 128, c * 128:(c + 1) * 128] = tile.T.astype(jnp.bfloat16)
-    xcopy(0, 0).start()
-    xcopy(0, 1).start()
     launch(0, 0)
     relay(1, 0)
-    finish(1, 0)
+    pl.semaphore_wait(plane_sem, 31)
+    for s in range(2):
+        xcopy(0, s).start()
+    for s in (0, 1, 2, 5, 3, 4):
+        xcopy(1, s).start()
     relay(0, 0)
     for s in range(2):
         xcopy(0, s).wait_recv()
     launch(0, 1)
+    finish(1, 0)
+    for s in (6, 7):
+        xcopy(1, s).start()
     finish(0, 0)
-    for s in range(8):
+    relay(0, 1)
+    for s in (0, 1, 2, 5, 3, 4, 6, 7):
         xcopy(1, s).wait_recv()
         d2d(1, 1, s).start()
-    relay(0, 1)
     finish(0, 1)
     for a, xp in ((1, 0), (0, 0), (1, 1), (0, 1)):
         for s in range(8):
             d2d(a, xp, s).wait_recv()
+    for copy in local:
+        copy.wait()
     for part in range(3):
         for dist in (1, 2, 3):
             along_z(dist, part).wait_send()
@@ -202,15 +218,22 @@
             d2d(a, xp, s).wait_send()
 
 
-def gather_blocks(q, k, v, o):
+def in_hbm(x):
+    return pltpu.with_memory_space_constraint(x, pltpu.HBM)
+
+
+def gather_blocks(q, k, v, o, hidden, gain, key_cache, value_cache):
     bf = jnp.bfloat16
     dma = pltpu.SemaphoreType.DMA
+    cache = jax.ShapeDtypeStruct(key_cache.shape, bf)
     return pl.pallas_call(
         gather_kernel,
         out_shape=(jax.ShapeDtypeStruct((4, 4, 1152, 256), bf),
-                   jax.ShapeDtypeStruct((4, 4, 128, 1152), bf)),
-        in_specs=[pl.BlockSpec(memory_space=pltpu.HBM)] * 4,
-        out_specs=[pl.BlockSpec(memory_space=pltpu.VMEM)] * 2,
+                   jax.ShapeDtypeStruct((4, 4, 128, 1152), bf),
+                   jax.ShapeDtypeStruct(hidden.shape, bf),
+                   jax.ShapeDtypeStruct(gain.shape, jnp.float32), cache, cache),
+        in_specs=[pl.BlockSpec(memory_space=pltpu.HBM)] * 8,
+        out_specs=[pl.BlockSpec(memory_space=pltpu.VMEM)] * 6,
         scratch_shapes=[
             pltpu.VMEM((4, 64, 1152), bf),
             pltpu.VMEM((256, 1152), bf),
@@ -218,15 +241,18 @@
             pltpu.VMEM((1152, 128), jnp.float32),
             dma((12,)), dma((4,)), dma((12,)), dma, dma((32,)), dma,
             dma((24,)), dma((24,)), dma((16,)), dma((16,)), dma((32,)), dma((32,)),
+            pltpu.SemaphoreType.REGULAR, dma((4,)),
         ],
         compiler_params=pltpu.CompilerParams(
             has_side_effects=True, vmem_limit_bytes=8 * 1024 * 1024),
         name="gather_blocks",
-    )(q, k, v, o)
-
-
-def attend_kernel(pos_ref, gq, go, hidden_ref, gain_ref, freq_ref, kc, vc, joined_ref, wo_ref, part_ref,
-                  out_sem):
+    )(*(in_hbm(x) for x in (q, k, v, o, hidden, gain, key_cache, value_cache)))
+
+
+def attend_kernel(pos_hbm, gq, go, hidden_ref, gain_ref, kc, vc, joined_ref, wo_ref, part_ref,
+                  pos_ref, pos_sem, out_sem):
+    pos_copy = pltpu.make_async_copy(pos_hbm, pos_ref, pos_sem)
+    pos_copy.start()
     copies = []
     for zs in range(4):
         for gs in range(4):
@@ -237,19 +263,21 @@
     f32, bf = jnp.float32, jnp.bfloat16
     hid = hidden_ref[...].astype(f32)
     mean_square = jnp.mean(hid * hid, axis=-1, keepdims=True)
-    normed = (hid * lax.rsqrt(mean_square + 1e-06) * gain_ref[...]).astype(bf)
+    gain = gain_ref[...].reshape(1, -1)
+    normed = (hid * lax.rsqrt(mean_square + 1e-06) * gain).astype(bf)
     proj = []
     for gs in range(4):
         acc = jnp.zeros((4, 256), f32)
         for zs in range(4):
             acc += jnp.dot(normed[:, zs * 1152:(zs + 1) * 1152], gq[zs, gs], preferred_element_type=f32)
         proj += [acc[:, :128], acc[:, 128:]]
+    pos_copy.wait()
     row = lax.broadcasted_iota(jnp.int32, (4, 128), 0)
     posf = jnp.zeros((4, 128), f32)
     for b in range(4):
         posf = jnp.where(row == b, pos_ref[b].astype(f32), posf)
-    angle = posf * freq_ref[...]
     lane = lax.broadcasted_iota(jnp.int32, (4, 128), 1)
+    angle = posf * jnp.exp((lane % 64).astype(f32) * (-2.0 / 128 * np.log(10000.0)))
     cosine = jnp.cos(angle)
     sine = jnp.where(lane < 64, -jnp.sin(angle), jnp.sin(angle))
 
@@ -295,22 +323,21 @@
     pltpu.make_async_copy(wo_ref, wo_ref, out_sem.at[1]).wait()
 
 
-def attend(positions, gq, go, hidden, norm_gain, key_cache, value_cache):
+def attend(positions, gathered):
     bf = jnp.bfloat16
     vmem = pl.BlockSpec(memory_space=pltpu.VMEM)
     hbm = pl.BlockSpec(memory_space=pltpu.HBM)
-    freq = 10000.0 ** (-2.0 * np.arange(64, dtype=np.float64) / 128)
-    freq = np.concatenate([freq, freq]).astype(np.float32)[None]
     return pl.pallas_call(
         attend_kernel,
         out_shape=(jax.ShapeDtypeStruct((4608, 1024), bf), jax.ShapeDtypeStruct((512, 4608), bf),
                    jax.ShapeDtypeStruct((8, 4, 576), jnp.float32)),
-        in_specs=[pl.BlockSpec(memory_space=pltpu.SMEM)] + [vmem] * 7,
+        in_specs=[hbm] + [vmem] * 6,
         out_specs=[hbm, hbm, vmem],
-        scratch_shapes=[pltpu.SemaphoreType.DMA((2,))],
+        scratch_shapes=[pltpu.SMEM((4,), jnp.int32), pltpu.SemaphoreType.DMA,
+                        pltpu.SemaphoreType.DMA((2,))],
         compiler_params=pltpu.CompilerParams(vmem_limit_bytes=20 * 1024 * 1024),
         name="attend",
-    )(positions, gq, go, hidden, norm_gain.reshape(1, -1), jnp.asarray(freq), key_cache, value_cache)
+    )(in_hbm(positions), *gathered)
 
 
 def norm_kernel(part_ref, gain_ref, out_ref, came, square, squares, p_send, p_recv, s_send, s_recv):
@@ -343,7 +370,7 @@
         sq(d).wait_recv()
         whole += squares[d - 1]
     scale = lax.rsqrt(whole[:, :1] / 4608.0 + 1e-06)
-    out_ref[...] = (total * scale * gain_ref[...]).astype(jnp.bfloat16)
+    out_ref[...] = (total * scale * gain_ref[...].reshape(1, -1)).astype(jnp.bfloat16)
     for d in range(1, 8):
         part(d).wait_send()
         sq(d).wait_send()
@@ -359,16 +386,17 @@
         out_specs=vmem,
         scratch_shapes=[pltpu.VMEM((7, 4, 576), jnp.float32), pltpu.VMEM((4, 128), jnp.float32),
                         pltpu.VMEM((7, 4, 128), jnp.float32), dma((7,)), dma((7,)), dma((7,)), dma((7,))],
-        compiler_params=pltpu.CompilerParams(has_side_effects=True, collective_id=1),
+        compiler_params=pltpu.CompilerParams(
+            has_side_effects=True, collective_id=1, vmem_limit_bytes=4 * 1024 * 1024),
         name="norm_sums",
-    )(part, post_gain.reshape(1, -1))
+    )(part, post_gain)
 
 
 def body(
     hidden, positions, key_cache, value_cache, norm_gain, q_proj, k_proj, v_proj, o_proj, post_gain
 ):
-    gq, go = gather_blocks(q_proj, k_proj, v_proj, o_proj)
-    joined, wo, part = attend(positions, gq, go, hidden, norm_gain, key_cache, value_cache)
+    gathered = gather_blocks(q_proj, k_proj, v_proj, o_proj, hidden, norm_gain, key_cache, value_cache)
+    joined, wo, part = attend(positions, gathered)
     return joined, wo, norm_sums(part, post_gain)
 
 

time: 159 us -> 105 us (0.66)
  Pallas kernels: 144 us -> 103 us
  local copies, waits for them, and re-layouts: 12.2 us -> 0.6 us
    pallas_call x1, Pallas kernels: 124 us -> 85.3 us  [gather_blocks(): pl.pallas_call(gather_kernel, out_shape=(jax.ShapeDtypeStruct((4, 4, 1152...]
    unnamed x23 -> x3, local copies, waits for them, and re-layouts: 10.9 us -> 0.6 us
    pallas_call x1, Pallas kernels: 7.42 us -> 5.38 us  [attend(): pl.pallas_call(attend_kernel, out_shape=(jax.ShapeDtypeStruct((4608, 1024...]
where the time goes in v3:
time: 105 us; the launch traced here: 104 us
  Pallas kernels  103 us (98%)
    pallas_call x1, Pallas kernels, gather_blocks(): pl.pallas_call(gather_kernel, out_shape=(jax.ShapeDtypeStruct((4, 4, 1152...  85.3 us
    pallas_call x1, Pallas kernels, norm_sums(): pl.pallas_call(norm_kernel, out_shape=jax.ShapeDtypeStruct((4, 576), jnp....  11.9 us
    pallas_call x1, Pallas kernels, attend(): pl.pallas_call(attend_kernel, out_shape=(jax.ShapeDtypeStruct((4608, 1024...  5.38 us

profile of v3, /device:TPU:1, one launch (start us, length us, event | category | flops | bytes accessed | tf_op | source)
XLA Modules:
  0.0 103.8 jit_solution(3705514193712061671)
XLA Ops:
  0.6 85.3 %gather_blocks.1 = (bf16[4,4,1152,256]{3,2,1,0:T(8,128)(2,1)S(1)}, bf16[4,4,128,1152]{3,2,1,0:T(8,128)(2,1)S(1)}, bf16[4,4608]{1,0:T(4,128)(2,1)S(1)}, f32[4608]...) custom-call(bf16[32,4608]{1,0:T(8,128)(2,1)} %q_ref.1, ...), custom_call_target="tpu_custom_call" | custom-call | tf_op jit(solution)/shard_map/gather_blocks/pallas_call | solution.py:229
  85.9 0.0 copy-start
  85.9 5.4 %attend.1 = (bf16[4608,1024]{1,0:T(8,128)(2,1)}, bf16[512,4608]{1,0:T(8,128)(2,1)}, f32[8,4,576]{2,1,0:T(4,128)S(1)}) custom-call(s32[4]{0:T(128)} %pos_hbm.1, bf16[4,4,1152,256]{3,2,1,0:T(8,128)(2,1)S(1)} %get-tuple-element.12.gq, bf16[4,4,128,1152]{3,2,1,0:T(8,128)(2,1)S(1)} %get-tuple-element.13.go, bf16[4,4608]{1,0:T(4,128)(2,1)S(1)} %get-tuple-element.14.hidden_ref, ...), custom_call_target="tpu_custom_call" | custom-call | tf_op jit(solution)/shard_map/attend/pallas_call | solution.py:330
  91.3 0.0 copy-done
  91.3 11.9 %norm_sums.1 = bf16[4,576]{1,0:T(4,128)(2,1)S(1)} custom-call(f32[8,4,576]{2,1,0:T(4,128)S(1)} %get-tuple-element.20.part_ref, f32[576]{0:T(1024)S(1)} %copy-done), custom_call_target="tpu_custom_call" | custom-call | tf_op jit(solution)/shard_map/norm_sums/pallas_call | solution.py:382
  103.2 0.6 copy.14
Async XLA Ops:
  85.9 5.4 %copy-start = (f32[576]{0:T(1024)S(1)}, f32[576]{0:T(1024)}, u32[]{:S(2)}) copy-start(f32[576]{0:T(1024)} %gain_ref.3) | copy-start | bytes 6916

commit v4 on v3

--- a/solution.py
+++ b/solution.py
@@ -9,6 +9,7 @@
 score_scale = 144.0 ** (-0.5)
 soft_cap = 50.0
 MESH = pl.DeviceIdType.MESH
+WO_SLICE = (0, 2, 3, 1)
 
 
 def remote(src, dst, ssem, rsem, device):
@@ -41,73 +42,96 @@
     def place(h_, z_, c_):
         return h_ * 8 + z_ * 2 + c_
 
+    zdest = 2 * h + z // 2
+    zdest = jnp.where(zdest == 0, 0, jnp.where(zdest == 1, 3, zdest - 1))
+    slot = (rep % 4) * 8 + tp
+
+    def o_slice(i, j):
+        p = (tp + i) % 8
+        gd = (g + j) % 4
+        src = o_ref.at[:, pl.ds(pl.multiple_of(p * 512 + gd * 128, 128), 128)]
+        return src, s1o.at[slot], place(gd // 2, zdest, gd % 2), p, o_send.at[4 * i + j], o_recv
+
+    def exchange(src, dst, dest_rep, dest_tp, ssem, rsem):
+        own = jnp.logical_and(dest_rep == rep, dest_tp == tp)
+
+        @pl.when(own)
+        def _():
+            pltpu.make_async_copy(src, dst, rsem).start()
+
+        @pl.when(jnp.logical_not(own))
+        def _():
+            remote(src, dst, ssem, rsem, (dest_rep, dest_tp)).start()
+
+    def exchange_done(src, dst, dest_rep, dest_tp, ssem, rsem):
+        own = jnp.logical_and(dest_rep == rep, dest_tp == tp)
+
+        @pl.when(jnp.logical_not(own))
+        def _():
+            remote(src, dst, ssem, rsem, (dest_rep, dest_tp)).wait_send()
+
+    for p in range(8):
+        for gd in range(4):
+            exchange(*o_slice(p, gd))
+
     width = s1q.shape[1]
     qrows, krows = q_ref.shape[0], k_ref.shape[0]
     parts = ((q_ref, 0, qrows), (k_ref, qrows, krows), (v_ref, qrows + krows, krows))
+
+    first_x = jnp.logical_and(h == 0, lo == 0)
+    last_x = jnp.logical_and(h == 1, lo == 1)
 
     def along_z(dist, part):
         zd = (z + dist) % 4
         ref, row, rows = parts[part]
         src = ref.at[:, pl.ds(pl.multiple_of(zd * width, width), width)]
+        if part == 0:
+            away, there, to_h, to_tp = last_x, qrows, 0, tp % 4
+        else:
+            away, there, to_h, to_tp = first_x, row - qrows, 1, 4 + tp % 4
+        row = pl.multiple_of(jnp.where(away, there, row), krows)
         dst = s1a.at[z, pl.ds(row, rows)]
-        if dist == 0:
-            return pltpu.make_async_copy(src, dst, a_recv.at[0])
-        return remote(src, dst, a_send.at[3 * dist + part], a_recv.at[dist], (place(h, zd, core), tp))
+        device = (place(jnp.where(away, to_h, h), zd, core), jnp.where(away, to_tp, tp))
+        return away, src, dst, remote(src, dst, a_send.at[3 * dist + part], a_recv.at[dist], device)
 
     for dist in (2, 1, 3, 0):
         for part in range(3):
-            along_z(dist, part).start()
+            away, src, dst, copy = along_z(dist, part)
+            if dist == 0:
+                pl.when(away)(copy.start)
+                pl.when(jnp.logical_not(away))(
+                    pltpu.make_async_copy(src, dst, a_recv.at[0]).start)
+            else:
+                copy.start()
 
     local = [pltpu.make_async_copy(src, dst, in_sem.at[i]) for i, (src, dst) in enumerate(
         ((hidden_ref, hidden_out), (gain_ref, gain_out), (kc_ref, kc_out), (vc_ref, vc_out)))]
     for copy in local:
         copy.start()
 
-    zdest = rep // 4
-    slot = (rep % 4) * 8 + tp
-
-    def o_slice(p, gd):
-        src = o_ref.at[:, pl.ds(p * 512 + gd * 128, 128)]
-        return src, s1o.at[slot], place(gd // 2, zdest, gd % 2), p, o_send.at[4 * p + gd], o_recv
-
-    def exchange(src, dst, dest_rep, dest_tp, ssem, rsem):
-        own = jnp.logical_and(dest_rep == rep, dest_tp == tp)
-
-        @pl.when(own)
-        def _():
-            pltpu.make_async_copy(src, dst, rsem).start()
-
-        @pl.when(jnp.logical_not(own))
-        def _():
-            remote(src, dst, ssem, rsem, (dest_rep, dest_tp)).start()
-
-    def exchange_done(src, dst, dest_rep, dest_tp, ssem, rsem):
-        own = jnp.logical_and(dest_rep == rep, dest_tp == tp)
-
-        @pl.when(jnp.logical_not(own))
-        def _():
-            remote(src, dst, ssem, rsem, (dest_rep, dest_tp)).wait_send()
-
-    for p in range(8):
-        for gd in range(4):
-            exchange(*o_slice(p, gd))
-
-    def to_owner(dist, part):
-        zs = (z + dist) % 4
-        _, row, rows = parts[part]
-        src = s1a.at[zs, pl.ds(row, rows)]
-        if part == 0:
-            dest, first = place(0, z, core), tp * rows
-        else:
-            dest, first = place(1, z, part - 1), core * 128 + tp * rows
-        dst = s1q.at[pl.ds(pl.multiple_of(first, rows), rows)]
-        return src, dst, dest, h * 4 + zs, b_send.at[3 * dist + part], q_recv
-
-    for dist in (0, 1, 3, 2):
-        came = s1a.at[(z + dist) % 4]
-        pltpu.make_async_copy(came, came, a_recv.at[(4 - dist) % 4]).wait()
-        for part in range(3):
-            exchange(*to_owner(dist, part))
+    def to_owners(dist, act):
+        zs = (tp + dist) % 4
+
+        def message(when, index, row, rows, dest, first, block):
+            dst = s1q.at[pl.ds(pl.multiple_of(first, rows), rows)]
+
+            @pl.when(when)
+            def _():
+                act(s1a.at[zs, pl.ds(row, rows)], dst, dest, block, b_send.at[4 * dist + index], q_recv)
+
+        y = tp % 4
+        message(jnp.logical_not(last_x), 0, 0, qrows, place(0, z, core), tp * qrows, h * 4 + zs)
+        message(first_x, 1, qrows, qrows, place(0, z, core), (4 + y) * qrows, 4 + zs)
+        for i in range(2):
+            message(jnp.logical_not(first_x), 1 + i, qrows + i * krows, krows, place(1, z, i),
+                    core * 128 + tp * krows, h * 4 + zs)
+            message(last_x, 3 * i, i * krows, krows, place(1, z, i), core * 128 + y * krows, zs)
+
+    for dist in (0, 2, 1, 3):
+        zs = (tp + dist) % 4
+        came = s1a.at[zs]
+        pltpu.make_async_copy(came, came, a_recv.at[(z + 4 - zs) % 4]).wait()
+        to_owners(dist, exchange)
 
     def chunk(a, zs, gs, half):
         return gathered[a].at[zs, gs, pl.ds(half * halves[a], halves[a])]
@@ -199,10 +223,14 @@
     for copy in local:
         copy.wait()
     for part in range(3):
-        for dist in (1, 2, 3):
-            along_z(dist, part).wait_send()
         for dist in range(4):
-            exchange_done(*to_owner(dist, part))
+            away, _, _, copy = along_z(dist, part)
+            if dist == 0:
+                pl.when(away)(copy.wait_send)
+            else:
+                copy.wait_send()
+    for dist in range(4):
+        to_owners(dist, exchange_done)
     for p in range(8):
         for gd in range(4):
             exchange_done(*o_slice(p, gd))
@@ -239,7 +267,7 @@
             pltpu.VMEM((256, 1152), bf),
             pltpu.VMEM((32, 36, 128), bf),
             pltpu.VMEM((1152, 128), jnp.float32),
-            dma((12,)), dma((4,)), dma((12,)), dma, dma((32,)), dma,
+            dma((12,)), dma((4,)), dma((16,)), dma, dma((32,)), dma,
             dma((24,)), dma((24,)), dma((16,)), dma((16,)), dma((32,)), dma((32,)),
             pltpu.SemaphoreType.REGULAR, dma((4,)),
         ],
@@ -257,7 +285,7 @@
     for zs in range(4):
         for gs in range(4):
             copies.append((gq.at[zs, gs], joined_ref.at[pl.ds(zs * 1152, 1152), pl.ds(gs * 256, 256)], 0))
-            copies.append((go.at[zs, gs], wo_ref.at[pl.ds(gs * 128, 128), pl.ds(zs * 1152, 1152)], 1))
+            copies.append((go.at[zs, gs], wo_ref.at[pl.ds(gs * 128, 128), pl.ds(WO_SLICE[zs] * 1152, 1152)], 1))
     for src, dst, i in copies:
         pltpu.make_async_copy(src, dst, out_sem.at[i]).start()
     f32, bf = jnp.float32, jnp.bfloat16
@@ -317,8 +345,8 @@
     att = jnp.concatenate([attention[i * 4:(i + 1) * 4] for i in range(4)], axis=1).astype(bf)
     for zs in range(4):
         part = jnp.dot(att, go[zs].reshape(512, 1152), preferred_element_type=f32)
-        part_ref[2 * zs] = part[:, :576]
-        part_ref[2 * zs + 1] = part[:, 576:]
+        part_ref[2 * WO_SLICE[zs]] = part[:, :576]
+        part_ref[2 * WO_SLICE[zs] + 1] = part[:, 576:]
     pltpu.make_async_copy(joined_ref, joined_ref, out_sem.at[0]).wait()
     pltpu.make_async_copy(wo_ref, wo_ref, out_sem.at[1]).wait()
 

time: 105 us -> 99.4 us (0.947)
  Pallas kernels: 103 us -> 97.8 us
    pallas_call x1, Pallas kernels: 85.3 us -> 82.3 us  [gather_blocks(): pl.pallas_call(gather_kernel, out_shape=(jax.ShapeDtypeStruct((4, 4, 1152...]
    pallas_call x1, Pallas kernels: 11.9 us -> 10.1 us  [norm_sums(): pl.pallas_call(norm_kernel, out_shape=jax.ShapeDtypeStruct((4, 576), jnp....]
where the time goes in v4:
time: 99.4 us; the launch traced here: 99 us
  Pallas kernels  97.8 us (98%)
    pallas_call x1, Pallas kernels, gather_blocks(): pl.pallas_call(gather_kernel, out_shape=(jax.ShapeDtypeStruct((4, 4, 1152...  82.3 us
    pallas_call x1, Pallas kernels, norm_sums(): pl.pallas_call(norm_kernel, out_shape=jax.ShapeDtypeStruct((4, 576), jnp....  10.1 us
    pallas_call x1, Pallas kernels, attend(): pl.pallas_call(attend_kernel, out_shape=(jax.ShapeDtypeStruct((4608, 1024...  5.38 us

profile of v4, /device:TPU:1, one launch (start us, length us, event | category | flops | bytes accessed | tf_op | source)
XLA Modules:
  0.0 99.0 jit_solution(15594833558508128085)
XLA Ops:
  0.6 82.3 %gather_blocks.1 = (bf16[4,4,1152,256]{3,2,1,0:T(8,128)(2,1)S(1)}, bf16[4,4,128,1152]{3,2,1,0:T(8,128)(2,1)S(1)}, bf16[4,4608]{1,0:T(4,128)(2,1)S(1)}, f32[4608]...) custom-call(bf16[32,4608]{1,0:T(8,128)(2,1)} %q_ref.1, ...), custom_call_target="tpu_custom_call" | custom-call | tf_op jit(solution)/shard_map/gather_blocks/pallas_call | solution.py:257
  83.0 0.0 copy-start
  83.0 5.4 %attend.1 = (bf16[4608,1024]{1,0:T(8,128)(2,1)}, bf16[512,4608]{1,0:T(8,128)(2,1)}, f32[8,4,576]{2,1,0:T(4,128)S(1)}) custom-call(s32[4]{0:T(128)} %pos_hbm.1, bf16[4,4,1152,256]{3,2,1,0:T(8,128)(2,1)S(1)} %get-tuple-element.12.gq, bf16[4,4,128,1152]{3,2,1,0:T(8,128)(2,1)S(1)} %get-tuple-element.13.go, bf16[4,4608]{1,0:T(4,128)(2,1)S(1)} %get-tuple-element.14.hidden_ref, ...), custom_call_target="tpu_custom_call" | custom-call | tf_op jit(solution)/shard_map/attend/pallas_call | solution.py:358
  88.4 0.0 copy-done
  88.4 10.1 %norm_sums.1 = bf16[4,576]{1,0:T(4,128)(2,1)S(1)} custom-call(f32[8,4,576]{2,1,0:T(4,128)S(1)} %get-tuple-element.20.part_ref, f32[576]{0:T(1024)S(1)} %copy-done), custom_call_target="tpu_custom_call" | custom-call | tf_op jit(solution)/shard_map/norm_sums/pallas_call | solution.py:410
  98.4 0.6 copy.14
Async XLA Ops:
  83.0 5.4 %copy-start = (f32[576]{0:T(1024)S(1)}, f32[576]{0:T(1024)}, u32[]{:S(2)}) copy-start(f32[576]{0:T(1024)} %gain_ref.3) | copy-start | bytes 6916

commit v5 on v4

--- a/solution.py
+++ b/solution.py
@@ -18,10 +18,12 @@
         device_id_type=MESH)
 
 
-def gather_kernel(q_ref, k_ref, v_ref, o_ref, hidden_ref, gain_ref, kc_ref, vc_ref,
-                  gq, go, hidden_out, gain_out, kc_out, vc_out, s1a, s1q, s1o, so,
+def gather_kernel(q_ref, k_ref, v_ref, o_ref, hidden_hbm, gain_hbm, kc_hbm, vc_hbm, pos_hbm, post_hbm,
+                  gq, go, out_ref,
+                  hidden_ref, gain_ref, kc, vc, pos_ref, post_ref, nrm, acc, rope, part_ref, parts_in, square,
+                  squares, s1a, s1q, s1o, so,
                   a_send, a_recv, b_send, q_recv, o_send, o_recv, z_send, z_recv, x_send, x_recv,
-                  d_send, d_recv, plane_sem, in_sem):
+                  d_send, d_recv, plane_sem, in_sem, p_send, p_recv, s_send, s_recv):
     rep = lax.axis_index("rep")
     tp = lax.axis_index("tp")
     h = rep // 8
@@ -105,9 +107,13 @@
                 copy.start()
 
     local = [pltpu.make_async_copy(src, dst, in_sem.at[i]) for i, (src, dst) in enumerate(
-        ((hidden_ref, hidden_out), (gain_ref, gain_out), (kc_ref, kc_out), (vc_ref, vc_out)))]
+        ((hidden_hbm, hidden_ref), (gain_hbm, gain_ref), (pos_hbm, pos_ref), (post_hbm, post_ref),
+         (kc_hbm, kc), (vc_hbm, vc)))]
     for copy in local:
         copy.start()
+    for copy in local:
+        copy.wait()
+    prepare(pos_ref, hidden_ref, gain_ref, nrm, acc, rope)
 
     def to_owners(dist, act):
         zs = (tp + dist) % 4
@@ -212,16 +218,33 @@
     for s in (6, 7):
         xcopy(1, s).start()
     finish(0, 0)
+
+    def project(xp, i):
+        zs = piece_z[i]
+        for s in (2 * i, 2 * i + 1):
+            d2d(0, xp, s).wait_recv()
+        for gs in (piece_g[xp], piece_g[xp] + 1 - 2 * core):
+            acc[gs] += jnp.dot(nrm[zs], gq[zs, gs], preferred_element_type=jnp.float32)
+
+    for i in range(4):
+        project(0, i)
     relay(0, 1)
+    project(1, 0)
     for s in (0, 1, 2, 5, 3, 4, 6, 7):
         xcopy(1, s).wait_recv()
         d2d(1, 1, s).start()
     finish(0, 1)
-    for a, xp in ((1, 0), (0, 0), (1, 1), (0, 1)):
+    for i in range(1, 4):
+        project(1, i)
+    att = attention(pos_ref, kc, vc, acc, rope)
+    for xp in range(2):
         for s in range(8):
-            d2d(a, xp, s).wait_recv()
-    for copy in local:
-        copy.wait()
+            d2d(1, xp, s).wait_recv()
+    for zs in range(4):
+        part = jnp.dot(att, go[zs].reshape(512, 1152), preferred_element_type=jnp.float32)
+        part_ref[2 * WO_SLICE[zs]] = part[:, :576]
+        part_ref[2 * WO_SLICE[zs] + 1] = part[:, 576:]
+    sum_and_norm(part_ref, post_ref, out_ref, parts_in, square, squares, p_send, p_recv, s_send, s_recv)
     for part in range(3):
         for dist in range(4):
             away, _, _, copy = along_z(dist, part)
@@ -250,64 +273,60 @@
     return pltpu.with_memory_space_constraint(x, pltpu.HBM)
 
 
-def gather_blocks(q, k, v, o, hidden, gain, key_cache, value_cache):
-    bf = jnp.bfloat16
+def gather_and_attend(q, k, v, o, hidden, gain, key_cache, value_cache, positions, post_gain):
+    bf, f32 = jnp.bfloat16, jnp.float32
     dma = pltpu.SemaphoreType.DMA
-    cache = jax.ShapeDtypeStruct(key_cache.shape, bf)
+    vmem = pltpu.VMEM
     return pl.pallas_call(
         gather_kernel,
         out_shape=(jax.ShapeDtypeStruct((4, 4, 1152, 256), bf),
                    jax.ShapeDtypeStruct((4, 4, 128, 1152), bf),
-                   jax.ShapeDtypeStruct(hidden.shape, bf),
-                   jax.ShapeDtypeStruct(gain.shape, jnp.float32), cache, cache),
-        in_specs=[pl.BlockSpec(memory_space=pltpu.HBM)] * 8,
-        out_specs=[pl.BlockSpec(memory_space=pltpu.VMEM)] * 6,
+                   jax.ShapeDtypeStruct((4, 576), bf)),
+        in_specs=[pl.BlockSpec(memory_space=pltpu.HBM)] * 10,
+        out_specs=[pl.BlockSpec(memory_space=vmem)] * 3,
         scratch_shapes=[
-            pltpu.VMEM((4, 64, 1152), bf),
-            pltpu.VMEM((256, 1152), bf),
-            pltpu.VMEM((32, 36, 128), bf),
-            pltpu.VMEM((1152, 128), jnp.float32),
+            vmem(hidden.shape, bf), vmem(gain.shape, f32), vmem(key_cache.shape, bf),
+            vmem(value_cache.shape, bf), pltpu.SMEM((4,), jnp.int32), vmem(post_gain.shape, f32),
+            vmem((4, 4, 1152), bf), vmem((4, 4, 256), f32), vmem((2, 4, 128), f32),
+            vmem((8, 4, 576), f32), vmem((7, 4, 576), f32), vmem((4, 128), f32), vmem((7, 4, 128), f32),
+            vmem((4, 64, 1152), bf), vmem((256, 1152), bf), vmem((32, 36, 128), bf),
+            vmem((1152, 128), f32),
             dma((12,)), dma((4,)), dma((16,)), dma, dma((32,)), dma,
             dma((24,)), dma((24,)), dma((16,)), dma((16,)), dma((32,)), dma((32,)),
-            pltpu.SemaphoreType.REGULAR, dma((4,)),
+            pltpu.SemaphoreType.REGULAR, dma((6,)), dma((7,)), dma((7,)), dma((7,)), dma((7,)),
         ],
         compiler_params=pltpu.CompilerParams(
-            has_side_effects=True, vmem_limit_bytes=8 * 1024 * 1024),
-        name="gather_blocks",
-    )(*(in_hbm(x) for x in (q, k, v, o, hidden, gain, key_cache, value_cache)))
-
-
-def attend_kernel(pos_hbm, gq, go, hidden_ref, gain_ref, kc, vc, joined_ref, wo_ref, part_ref,
-                  pos_ref, pos_sem, out_sem):
-    pos_copy = pltpu.make_async_copy(pos_hbm, pos_ref, pos_sem)
-    pos_copy.start()
-    copies = []
-    for zs in range(4):
-        for gs in range(4):
-            copies.append((gq.at[zs, gs], joined_ref.at[pl.ds(zs * 1152, 1152), pl.ds(gs * 256, 256)], 0))
-            copies.append((go.at[zs, gs], wo_ref.at[pl.ds(gs * 128, 128), pl.ds(WO_SLICE[zs] * 1152, 1152)], 1))
-    for src, dst, i in copies:
-        pltpu.make_async_copy(src, dst, out_sem.at[i]).start()
-    f32, bf = jnp.float32, jnp.bfloat16
+            has_side_effects=True, vmem_limit_bytes=16 * 1024 * 1024),
+        name="gather_and_attend",
+    )(*(in_hbm(x) for x in (q, k, v, o, hidden, gain, key_cache, value_cache, positions, post_gain)))
+
+
+def prepare(pos_ref, hidden_ref, gain_ref, nrm, acc, rope):
+    f32 = jnp.float32
     hid = hidden_ref[...].astype(f32)
     mean_square = jnp.mean(hid * hid, axis=-1, keepdims=True)
     gain = gain_ref[...].reshape(1, -1)
-    normed = (hid * lax.rsqrt(mean_square + 1e-06) * gain).astype(bf)
-    proj = []
-    for gs in range(4):
-        acc = jnp.zeros((4, 256), f32)
-        for zs in range(4):
-            acc += jnp.dot(normed[:, zs * 1152:(zs + 1) * 1152], gq[zs, gs], preferred_element_type=f32)
-        proj += [acc[:, :128], acc[:, 128:]]
-    pos_copy.wait()
+    normed = (hid * lax.rsqrt(mean_square + 1e-06) * gain).astype(jnp.bfloat16)
+    for zs in range(4):
+        nrm[zs] = normed[:, zs * 1152:(zs + 1) * 1152]
+    acc[...] = jnp.zeros_like(acc)
     row = lax.broadcasted_iota(jnp.int32, (4, 128), 0)
     posf = jnp.zeros((4, 128), f32)
     for b in range(4):
         posf = jnp.where(row == b, pos_ref[b].astype(f32), posf)
     lane = lax.broadcasted_iota(jnp.int32, (4, 128), 1)
     angle = posf * jnp.exp((lane % 64).astype(f32) * (-2.0 / 128 * np.log(10000.0)))
-    cosine = jnp.cos(angle)
-    sine = jnp.where(lane < 64, -jnp.sin(angle), jnp.sin(angle))
+    rope[0] = jnp.cos(angle)
+    rope[1] = jnp.where(lane < 64, -jnp.sin(angle), jnp.sin(angle))
+
+
+def attention(pos_ref, kc, vc, acc, rope):
+    f32, bf = jnp.float32, jnp.bfloat16
+    proj = []
+    for gs in range(4):
+        both = acc[gs]
+        proj += [both[:, :128], both[:, 128:]]
+    cosine, sine = rope[0], rope[1]
 
     def rotate(x):
         swapped = jnp.concatenate([x[:, 64:], x[:, :64]], axis=1)
@@ -337,48 +356,49 @@
     self_raw = jnp.exp(soft_cap * jnp.tanh(self_score / soft_cap))
     denom = jnp.sum(raw, axis=-1, keepdims=True) + self_raw
     weights = (raw / denom).astype(bf).astype(f32)
-    attention = (self_raw / denom).astype(bf).astype(f32) * values_new
+    mixed = (self_raw / denom).astype(bf).astype(f32) * values_new
     for kv in range(2):
         for b in range(4):
             w = jnp.where(owner == kv * 4 + b, weights, 0.0).astype(bf)
-            attention += jnp.dot(w, vc[b, kv], preferred_element_type=f32)
-    att = jnp.concatenate([attention[i * 4:(i + 1) * 4] for i in range(4)], axis=1).astype(bf)
+            mixed += jnp.dot(w, vc[b, kv], preferred_element_type=f32)
+    return jnp.concatenate([mixed[i * 4:(i + 1) * 4] for i in range(4)], axis=1).astype(bf)
+
+
+def write_kernel(gq, go, joined_ref, wo_ref, out_sem):
     for zs in range(4):
-        part = jnp.dot(att, go[zs].reshape(512, 1152), preferred_element_type=f32)
-        part_ref[2 * WO_SLICE[zs]] = part[:, :576]
-        part_ref[2 * WO_SLICE[zs] + 1] = part[:, 576:]
+        for gs in range(4):
+            pltpu.make_async_copy(
+                gq.at[zs, gs], joined_ref.at[pl.ds(zs * 1152, 1152), pl.ds(gs * 256, 256)],
+                out_sem.at[0]).start()
+            pltpu.make_async_copy(
+                go.at[zs, gs], wo_ref.at[pl.ds(gs * 128, 128), pl.ds(WO_SLICE[zs] * 1152, 1152)],
+                out_sem.at[1]).start()
     pltpu.make_async_copy(joined_ref, joined_ref, out_sem.at[0]).wait()
     pltpu.make_async_copy(wo_ref, wo_ref, out_sem.at[1]).wait()
 
 
-def attend(positions, gathered):
+def write_out(gq, go):
     bf = jnp.bfloat16
     vmem = pl.BlockSpec(memory_space=pltpu.VMEM)
     hbm = pl.BlockSpec(memory_space=pltpu.HBM)
     return pl.pallas_call(
-        attend_kernel,
-        out_shape=(jax.ShapeDtypeStruct((4608, 1024), bf), jax.ShapeDtypeStruct((512, 4608), bf),
-                   jax.ShapeDtypeStruct((8, 4, 576), jnp.float32)),
-        in_specs=[hbm] + [vmem] * 6,
-        out_specs=[hbm, hbm, vmem],
-        scratch_shapes=[pltpu.SMEM((4,), jnp.int32), pltpu.SemaphoreType.DMA,
-                        pltpu.SemaphoreType.DMA((2,))],
-        compiler_params=pltpu.CompilerParams(vmem_limit_bytes=20 * 1024 * 1024),
-        name="attend",
-    )(in_hbm(positions), *gathered)
-
-
-def norm_kernel(part_ref, gain_ref, out_ref, came, square, squares, p_send, p_recv, s_send, s_recv):
+        write_kernel,
+        out_shape=(jax.ShapeDtypeStruct((4608, 1024), bf), jax.ShapeDtypeStruct((512, 4608), bf)),
+        in_specs=[vmem, vmem],
+        out_specs=[hbm, hbm],
+        scratch_shapes=[pltpu.SemaphoreType.DMA((2,))],
+        compiler_params=pltpu.CompilerParams(vmem_limit_bytes=16 * 1024 * 1024),
+        name="write_out",
+    )(gq, go)
+
+
+def sum_and_norm(part_ref, gain_ref, out_ref, parts_in, square, squares, p_send, p_recv, s_send, s_recv):
     rep = lax.axis_index("rep")
     tp = lax.axis_index("tp")
-    barrier = pltpu.get_barrier_semaphore()
-    for d in range(1, 8):
-        pl.semaphore_signal(barrier, inc=1, device_id=(rep, (tp + d) % 8), device_id_type=MESH)
-    pl.semaphore_wait(barrier, 7)
 
     def part(d):
         to = (tp + d) % 8
-        return remote(part_ref.at[to], came.at[d - 1], p_send.at[d - 1], p_recv.at[d - 1], (rep, to))
+        return remote(part_ref.at[to], parts_in.at[d - 1], p_send.at[d - 1], p_recv.at[d - 1], (rep, to))
 
     def sq(d):
         return remote(square, squares.at[d - 1], s_send.at[d - 1], s_recv.at[d - 1],
@@ -389,7 +409,7 @@
     total = part_ref[tp]
     for d in range(1, 8):
         part(d).wait_recv()
-        total += came[d - 1]
+        total += parts_in[d - 1]
     square[...] = jnp.broadcast_to(jnp.sum(total * total, axis=-1, keepdims=True), square.shape)
     for d in range(1, 8):
         sq(d).start()
@@ -404,28 +424,13 @@
         sq(d).wait_send()
 
 
-def norm_sums(part, post_gain):
-    vmem = pl.BlockSpec(memory_space=pltpu.VMEM)
-    dma = pltpu.SemaphoreType.DMA
-    return pl.pallas_call(
-        norm_kernel,
-        out_shape=jax.ShapeDtypeStruct((4, 576), jnp.bfloat16),
-        in_specs=[vmem, vmem],
-        out_specs=vmem,
-        scratch_shapes=[pltpu.VMEM((7, 4, 576), jnp.float32), pltpu.VMEM((4, 128), jnp.float32),
-                        pltpu.VMEM((7, 4, 128), jnp.float32), dma((7,)), dma((7,)), dma((7,)), dma((7,))],
-        compiler_params=pltpu.CompilerParams(
-            has_side_effects=True, collective_id=1, vmem_limit_bytes=4 * 1024 * 1024),
-        name="norm_sums",
-    )(part, post_gain)
-
-
 def body(
     hidden, positions, key_cache, value_cache, norm_gain, q_proj, k_proj, v_proj, o_proj, post_gain
 ):
-    gathered = gather_blocks(q_proj, k_proj, v_proj, o_proj, hidden, norm_gain, key_cache, value_cache)
-    joined, wo, part = attend(positions, gathered)
-    return joined, wo, norm_sums(part, post_gain)
+    gq, go, attn_out = gather_and_attend(
+        q_proj, k_proj, v_proj, o_proj, hidden, norm_gain, key_cache, value_cache, positions, post_gain)
+    joined, wo = write_out(gq, go)
+    return joined, wo, attn_out
 
 
 def solution(mesh):

time: 99.4 us -> 98.9 us (level)
    pallas_call x3 -> x2, Pallas kernels: 97.8 us -> 97.5 us  [the longest x1 92.5 us: gather_and_attend(): pl.pallas_call(gather_kernel, out_shape=(jax.ShapeDtypeStruct((4, 4, 1152...]
where the time goes in v5:
time: 98.9 us; the launch traced here: 98.8 us
  Pallas kernels  97.5 us (99%)
    pallas_call x1, Pallas kernels, gather_and_attend(): pl.pallas_call(gather_kernel, out_shape=(jax.ShapeDtypeStruct((4, 4, 1152...  92.5 us
    pallas_call x1, Pallas kernels, write_out(): pl.pallas_call(write_kernel, out_shape=(jax.ShapeDtypeStruct((4608, 1024)...  5.02 us

profile of v5, /device:TPU:1, one launch (start us, length us, event | category | flops | bytes accessed | tf_op | source)
XLA Modules:
  0.0 98.8 jit_solution(6293828054277984236)
XLA Ops:
  0.6 92.5 %gather_and_attend.1 = (bf16[4,4,1152,256]{3,2,1,0:T(8,128)(2,1)S(1)}, bf16[4,4,128,1152]{3,2,1,0:T(8,128)(2,1)S(1)}, bf16[4,576]{1,0:T(4,128)(2,1)S(1)}) custom-call(bf16[32,4608]{1,0:T(8,128)(2,1)} %q_ref.1, bf16[16,4608]{1,0:T(8,128)(2,1)} %k_ref.1, bf16[16,4608]{1,0:T(8,128)(2,1)} %v_ref.1, bf16[36,4096]{1,0:T(8,128)(2,1)} %o_ref.1, ...), custom_call_target="tpu_custom_call" | custom-call | tf_op jit(solution)/shard_map/gather_and_attend/pallas_call | solution.py:280
  93.1 5.0 %write_out.1 = (bf16[4608,1024]{1,0:T(8,128)(2,1)}, bf16[512,4608]{1,0:T(8,128)(2,1)}) custom-call(bf16[4,4,1152,256]{3,2,1,0:T(8,128)(2,1)S(1)} %get-tuple-element.8.gq, bf16[4,4,128,1152]{3,2,1,0:T(8,128)(2,1)S(1)} %get-tuple-element.9.go), custom_call_target="tpu_custom_call" | custom-call | tf_op jit(solution)/shard_map/write_out/pallas_call | solution.py:384
  98.2 0.6 copy.14

commit v6 on v5

--- a/solution.py
+++ b/solution.py
@@ -23,7 +23,7 @@
                   hidden_ref, gain_ref, kc, vc, pos_ref, post_ref, nrm, acc, rope, part_ref, parts_in, square,
                   squares, s1a, s1q, s1o, so,
                   a_send, a_recv, b_send, q_recv, o_send, o_recv, z_send, z_recv, x_send, x_recv,
-                  d_send, d_recv, plane_sem, in_sem, p_send, p_recv, s_send, s_recv):
+                  d_send, d_recv, row_sem, in_sem, p_send, p_recv, s_send, s_recv):
     rep = lax.axis_index("rep")
     tp = lax.axis_index("tp")
     h = rep // 8
@@ -32,7 +32,6 @@
     lo = tp // 4
     g = 2 * h + core
     gpar = 2 * (1 - h) + core
-    rep_in_plane = g
     zp = (z + 1) % 4
     zm = (z + 3) % 4
     zo = (z + 2) % 4
@@ -43,6 +42,16 @@
 
     def place(h_, z_, c_):
         return h_ * 8 + z_ * 2 + c_
+
+    barrier = pltpu.get_barrier_semaphore()
+    pair = z + 1 - 2 * (z % 2)
+    greeted = [((z_ + 2) % 4, h_, core, tp_) for z_ in (pair, z)
+               for h_, tp_ in ((1 - h, (tp + 4) % 8), (h, tp))]
+    greeted += [(z_, (g + a) % 4 // 2, (g + a) % 2, (tp + b) % 8) for z_ in (pair, z)
+                for a in (2, 3, 1, 0) for b in (6, 2, 5, 7, 1, 3, 4, 0)][:-1]
+    for z_, h_, c_, tp_ in greeted:
+        pl.semaphore_signal(barrier, inc=1, device_id=(place(h_, z_, c_), tp_), device_id_type=MESH)
+    pl.semaphore_wait(barrier, len(greeted))
 
     zdest = 2 * h + z // 2
     zdest = jnp.where(zdest == 0, 0, jnp.where(zdest == 1, 3, zdest - 1))
@@ -194,18 +203,21 @@
     for b in range(9):
         go[z, g, :, b * 128:(b + 1) * 128] = so[b * 128:(b + 1) * 128, :].T.astype(jnp.bfloat16)
     launch(1, 0)
+    for dist in range(4):
+        to_owners(dist, exchange_done)
+    for i in range(1, 8):
+        peer = (2 * h + lo + i // 2) % 4
+        pl.semaphore_signal(
+            row_sem, inc=1, device_id_type=MESH,
+            device_id=(place(peer // 2, z, (core + i) % 2), (peer % 2) * 4 + tp % 4))
     pltpu.make_async_copy(s1q, s1q, q_recv).wait()
-    for i in range(1, 32):
-        peer = (rep_in_plane + i // 8) % 4
-        pl.semaphore_signal(plane_sem, inc=1, device_id=(place(peer // 2, z, peer % 2), (tp + i) % 8),
-                            device_id_type=MESH)
     for b in range(9):
         for c in range(2):
             tile = s1q[c * 128:(c + 1) * 128, b * 128:(b + 1) * 128].astype(jnp.float32)
             gq[z, g, b * 128:(b + 1) * 128, c * 128:(c + 1) * 128] = tile.T.astype(jnp.bfloat16)
     launch(0, 0)
     relay(1, 0)
-    pl.semaphore_wait(plane_sem, 31)
+    pl.semaphore_wait(row_sem, 7)
     for s in range(2):
         xcopy(0, s).start()
     for s in (0, 1, 2, 5, 3, 4):
@@ -252,8 +264,6 @@
                 pl.when(away)(copy.wait_send)
             else:
                 copy.wait_send()
-    for dist in range(4):
-        to_owners(dist, exchange_done)
     for p in range(8):
         for gd in range(4):
             exchange_done(*o_slice(p, gd))
@@ -296,7 +306,7 @@
             pltpu.SemaphoreType.REGULAR, dma((6,)), dma((7,)), dma((7,)), dma((7,)), dma((7,)),
         ],
         compiler_params=pltpu.CompilerParams(
-            has_side_effects=True, vmem_limit_bytes=16 * 1024 * 1024),
+            has_side_effects=True, collective_id=0, vmem_limit_bytes=16 * 1024 * 1024),
         name="gather_and_attend",
     )(*(in_hbm(x) for x in (q, k, v, o, hidden, gain, key_cache, value_cache, positions, post_gain)))
 
@@ -364,7 +374,8 @@
     return jnp.concatenate([mixed[i * 4:(i + 1) * 4] for i in range(4)], axis=1).astype(bf)
 
 
-def write_kernel(gq, go, joined_ref, wo_ref, out_sem):
+def write_kernel(gq, go, small, joined_ref, wo_ref, small_ref, out_sem):
+    pltpu.make_async_copy(small, small_ref, out_sem.at[2]).start()
     for zs in range(4):
         for gs in range(4):
             pltpu.make_async_copy(
@@ -375,21 +386,23 @@
                 out_sem.at[1]).start()
     pltpu.make_async_copy(joined_ref, joined_ref, out_sem.at[0]).wait()
     pltpu.make_async_copy(wo_ref, wo_ref, out_sem.at[1]).wait()
-
-
-def write_out(gq, go):
+    pltpu.make_async_copy(small, small_ref, out_sem.at[2]).wait()
+
+
+def write_out(gq, go, small):
     bf = jnp.bfloat16
     vmem = pl.BlockSpec(memory_space=pltpu.VMEM)
     hbm = pl.BlockSpec(memory_space=pltpu.HBM)
     return pl.pallas_call(
         write_kernel,
-        out_shape=(jax.ShapeDtypeStruct((4608, 1024), bf), jax.ShapeDtypeStruct((512, 4608), bf)),
-        in_specs=[vmem, vmem],
-        out_specs=[hbm, hbm],
-        scratch_shapes=[pltpu.SemaphoreType.DMA((2,))],
+        out_shape=(jax.ShapeDtypeStruct((4608, 1024), bf), jax.ShapeDtypeStruct((512, 4608), bf),
+                   jax.ShapeDtypeStruct(small.shape, bf)),
+        in_specs=[vmem, vmem, vmem],
+        out_specs=[hbm, hbm, hbm],
+        scratch_shapes=[pltpu.SemaphoreType.DMA((3,))],
         compiler_params=pltpu.CompilerParams(vmem_limit_bytes=16 * 1024 * 1024),
         name="write_out",
-    )(gq, go)
+    )(gq, go, small)
 
 
 def sum_and_norm(part_ref, gain_ref, out_ref, parts_in, square, squares, p_send, p_recv, s_send, s_recv):
@@ -429,8 +442,7 @@
 ):
     gq, go, attn_out = gather_and_attend(
         q_proj, k_proj, v_proj, o_proj, hidden, norm_gain, key_cache, value_cache, positions, post_gain)
-    joined, wo = write_out(gq, go)
-    return joined, wo, attn_out
+    return write_out(gq, go, attn_out)
 
 
 def solution(mesh):

time: 98.9 us -> 92.9 us (0.939)
  Pallas kernels: 97.5 us -> 92.2 us
    pallas_call x1, Pallas kernels: 92.5 us -> 87.1 us  [gather_and_attend(): pl.pallas_call(gather_kernel, out_shape=(jax.ShapeDtypeStruct((4, 4, 1152...]
where the time goes in v6:
time: 92.9 us; the launch traced here: 92.8 us
  Pallas kernels  92.2 us (99%)
    pallas_call x1, Pallas kernels, gather_and_attend(): pl.pallas_call(gather_kernel, out_shape=(jax.ShapeDtypeStruct((4, 4, 1152...  87.1 us
    pallas_call x1, Pallas kernels, write_out(): pl.pallas_call(write_kernel, out_shape=(jax.ShapeDtypeStruct((4608, 1024)...  5.04 us

profile of v6, /device:TPU:1, one launch (start us, length us, event | category | flops | bytes accessed | tf_op | source)
XLA Modules:
  0.0 92.8 jit_solution(8391796431274483329)
XLA Ops:
  0.6 87.1 %gather_and_attend.1 = (bf16[4,4,1152,256]{3,2,1,0:T(8,128)(2,1)S(1)}, bf16[4,4,128,1152]{3,2,1,0:T(8,128)(2,1)S(1)}, bf16[4,576]{1,0:T(4,128)(2,1)S(1)}) custom-call(bf16[32,4608]{1,0:T(8,128)(2,1)} %q_ref.1, bf16[16,4608]{1,0:T(8,128)(2,1)} %k_ref.1, bf16[16,4608]{1,0:T(8,128)(2,1)} %v_ref.1, bf16[36,4096]{1,0:T(8,128)(2,1)} %o_ref.1, ...), custom_call_target="tpu_custom_call" | custom-call | tf_op jit(solution)/shard_map/gather_and_attend/pallas_call | solution.py:290
  87.8 5.0 %write_out.1 = (bf16[4608,1024]{1,0:T(8,128)(2,1)}, bf16[512,4608]{1,0:T(8,128)(2,1)}, bf16[4,576]{1,0:T(4,128)(2,1)}) custom-call(bf16[4,4,1152,256]{3,2,1,0:T(8,128)(2,1)S(1)} %get-tuple-element.6.gq, bf16[4,4,128,1152]{3,2,1,0:T(8,128)(2,1)S(1)} %get-tuple-element.7.go, bf16[4,576]{1,0:T(4,128)(2,1)S(1)} %get-tuple-element.8.small), custom_call_target="tpu_custom_call" | custom-call | tf_op jit(solution)/shard_map/write_out/pallas_call | solution.py:396

commit v7 on v6

--- a/solution.py
+++ b/solution.py
@@ -20,10 +20,9 @@
 
 def gather_kernel(q_ref, k_ref, v_ref, o_ref, hidden_hbm, gain_hbm, kc_hbm, vc_hbm, pos_hbm, post_hbm,
                   gq, go, out_ref,
-                  hidden_ref, gain_ref, kc, vc, pos_ref, post_ref, nrm, acc, rope, part_ref, parts_in, square,
-                  squares, s1a, s1q, s1o, so,
+                  hidden_ref, gain_ref, kc, vc, pos_ref, post_ref, nrm, acc, rope, part_ref, parts_in, s1a, s1q, s1o, so,
                   a_send, a_recv, b_send, q_recv, o_send, o_recv, z_send, z_recv, x_send, x_recv,
-                  d_send, d_recv, row_sem, in_sem, p_send, p_recv, s_send, s_recv):
+                  d_send, d_recv, row_sem, in_sem, p_send, p_recv):
     rep = lax.axis_index("rep")
     tp = lax.axis_index("tp")
     h = rep // 8
@@ -151,8 +150,30 @@
     def chunk(a, zs, gs, half):
         return gathered[a].at[zs, gs, pl.ds(half * halves[a], halves[a])]
 
+    early = 192
+    late = (gq.shape[2] - early) // 2
+
+    def ring_chunk(a, xp, zs, half):
+        if a == 0 and xp == 1:
+            return gq.at[zs, gpar, pl.ds(early + half * late, late)]
+        return chunk(a, zs, piece_g[xp], half)
+
+    def early_rows(i, gs):
+        return gq.at[piece_z[i], gs, pl.ds(0, early)]
+
+    def xearly(i):
+        c = early_rows(i, g)
+        return remote(c, c, x_send.at[2 + i], x_recv.at[2 + i], (place(1 - h, z, core), tp))
+
+    def dearly(i):
+        c = early_rows(i, gpar)
+        return remote(c, c, d_send.at[32 + i], d_recv.at[32 + i], (place(h, z, 1 - core), tp))
+
     def d2d(a, xp, s):
-        c = chunk(a, piece_z[s // 2], piece_g[xp], s % 2)
+        if s < 2:
+            c = chunk(a, z, piece_g[xp], s)
+        else:
+            c = ring_chunk(a, xp, piece_z[s // 2], s % 2)
         i = (a * 2 + xp) * 8 + s
         return remote(c, c, d_send.at[i], d_recv.at[i], (place(h, z, 1 - core), tp))
 
@@ -161,7 +182,7 @@
 
     def zcopy(a, xp, i):
         zs, half, to = ((z, 0, up), (z, 1, up), (z, 0, down), (z, 1, down), (zm, 0, up), (zp, 1, down))[i]
-        c = chunk(a, zs, piece_g[xp], half)
+        c = ring_chunk(a, xp, zs, half)
         j = (a * 2 + xp) * 6 + i
         return remote(c, c, z_send.at[j], z_recv.at[j], to)
 
@@ -210,53 +231,72 @@
         pl.semaphore_signal(
             row_sem, inc=1, device_id_type=MESH,
             device_id=(place(peer // 2, z, (core + i) % 2), (peer % 2) * 4 + tp % 4))
+    for s in range(2):
+        xcopy(1, s).start()
     pltpu.make_async_copy(s1q, s1q, q_recv).wait()
     for b in range(9):
         for c in range(2):
             tile = s1q[c * 128:(c + 1) * 128, b * 128:(b + 1) * 128].astype(jnp.float32)
             gq[z, g, b * 128:(b + 1) * 128, c * 128:(c + 1) * 128] = tile.T.astype(jnp.bfloat16)
     launch(0, 0)
-    relay(1, 0)
     pl.semaphore_wait(row_sem, 7)
     for s in range(2):
         xcopy(0, s).start()
-    for s in (0, 1, 2, 5, 3, 4):
+    relay(1, 0)
+    for s in (2, 5, 3, 4):
         xcopy(1, s).start()
     relay(0, 0)
+    for i in (1, 2):
+        xearly(i).start()
     for s in range(2):
         xcopy(0, s).wait_recv()
     launch(0, 1)
     finish(1, 0)
+    finish(0, 0)
+    xearly(3).start()
     for s in (6, 7):
         xcopy(1, s).start()
-    finish(0, 0)
 
     def project(xp, i):
-        zs = piece_z[i]
+        def add(gs):
+            acc[gs] += jnp.dot(nrm[piece_z[i]], gq[piece_z[i], gs], preferred_element_type=jnp.float32)
+
+        add(piece_g[xp])
         for s in (2 * i, 2 * i + 1):
             d2d(0, xp, s).wait_recv()
-        for gs in (piece_g[xp], piece_g[xp] + 1 - 2 * core):
-            acc[gs] += jnp.dot(nrm[zs], gq[zs, gs], preferred_element_type=jnp.float32)
+        if xp == 1 and i > 0:
+            dearly(i).wait_recv()
+        add(piece_g[xp] + 1 - 2 * core)
 
     for i in range(4):
         project(0, i)
     relay(0, 1)
     project(1, 0)
-    for s in (0, 1, 2, 5, 3, 4, 6, 7):
+    for s in (0, 1, 2, 5, 3, 4):
         xcopy(1, s).wait_recv()
         d2d(1, 1, s).start()
+    for i in (1, 2):
+        xearly(i).wait_recv()
+        dearly(i).start()
+    project(1, 1)
+    project(1, 2)
+    xearly(3).wait_recv()
+    dearly(3).start()
     finish(0, 1)
-    for i in range(1, 4):
-        project(1, i)
+    project(1, 3)
+    for s in (6, 7):
+        xcopy(1, s).wait_recv()
+        d2d(1, 1, s).start()
     att = attention(pos_ref, kc, vc, acc, rope)
     for xp in range(2):
         for s in range(8):
             d2d(1, xp, s).wait_recv()
     for zs in range(4):
         part = jnp.dot(att, go[zs].reshape(512, 1152), preferred_element_type=jnp.float32)
+        part = part.astype(jnp.bfloat16)
         part_ref[2 * WO_SLICE[zs]] = part[:, :576]
         part_ref[2 * WO_SLICE[zs] + 1] = part[:, 576:]
-    sum_and_norm(part_ref, post_ref, out_ref, parts_in, square, squares, p_send, p_recv, s_send, s_recv)
+    sum_and_norm(part_ref, post_ref, out_ref, parts_in, p_send, p_recv)
     for part in range(3):
         for dist in range(4):
             away, _, _, copy = along_z(dist, part)
@@ -271,6 +311,9 @@
         xcopy(0, s).wait_send()
     for s in range(8):
         xcopy(1, s).wait_send()
+    for i in range(1, 4):
+        xearly(i).wait_send()
+        dearly(i).wait_send()
     for a, xp in ((1, 0), (0, 0), (1, 1), (0, 1)):
         if (a, xp) != (1, 1):
             for i in range(6):
@@ -298,12 +341,12 @@
             vmem(hidden.shape, bf), vmem(gain.shape, f32), vmem(key_cache.shape, bf),
             vmem(value_cache.shape, bf), pltpu.SMEM((4,), jnp.int32), vmem(post_gain.shape, f32),
             vmem((4, 4, 1152), bf), vmem((4, 4, 256), f32), vmem((2, 4, 128), f32),
-            vmem((8, 4, 576), f32), vmem((7, 4, 576), f32), vmem((4, 128), f32), vmem((7, 4, 128), f32),
+            vmem((8, 4, 576), bf), vmem((7, 8, 4, 576), bf),
             vmem((4, 64, 1152), bf), vmem((256, 1152), bf), vmem((32, 36, 128), bf),
             vmem((1152, 128), f32),
             dma((12,)), dma((4,)), dma((16,)), dma, dma((32,)), dma,
-            dma((24,)), dma((24,)), dma((16,)), dma((16,)), dma((32,)), dma((32,)),
-            pltpu.SemaphoreType.REGULAR, dma((6,)), dma((7,)), dma((7,)), dma((7,)), dma((7,)),
+            dma((24,)), dma((24,)), dma((16,)), dma((16,)), dma((36,)), dma((36,)),
+            pltpu.SemaphoreType.REGULAR, dma((6,)), dma((7,)), dma((7,)),
         ],
         compiler_params=pltpu.CompilerParams(
             has_side_effects=True, collective_id=0, vmem_limit_bytes=16 * 1024 * 1024),
@@ -405,36 +448,28 @@
     )(gq, go, small)
 
 
-def sum_and_norm(part_ref, gain_ref, out_ref, parts_in, square, squares, p_send, p_recv, s_send, s_recv):
+def sum_and_norm(part_ref, gain_ref, out_ref, parts_in, p_send, p_recv):
+    f32 = jnp.float32
     rep = lax.axis_index("rep")
     tp = lax.axis_index("tp")
 
     def part(d):
-        to = (tp + d) % 8
-        return remote(part_ref.at[to], parts_in.at[d - 1], p_send.at[d - 1], p_recv.at[d - 1], (rep, to))
-
-    def sq(d):
-        return remote(square, squares.at[d - 1], s_send.at[d - 1], s_recv.at[d - 1],
+        return remote(part_ref, parts_in.at[d - 1], p_send.at[d - 1], p_recv.at[d - 1],
                       (rep, (tp + d) % 8))
 
-    for d in range(1, 8):
+    for d in (6, 2, 5, 7, 1, 3, 4):
         part(d).start()
-    total = part_ref[tp]
-    for d in range(1, 8):
+    total = part_ref[...].astype(f32)
+    own = part_ref[tp].astype(f32)
+    for d in (4, 1, 3, 7, 5, 2, 6):
         part(d).wait_recv()
-        total += parts_in[d - 1]
-    square[...] = jnp.broadcast_to(jnp.sum(total * total, axis=-1, keepdims=True), square.shape)
-    for d in range(1, 8):
-        sq(d).start()
-    whole = square[...]
-    for d in range(1, 8):
-        sq(d).wait_recv()
-        whole += squares[d - 1]
-    scale = lax.rsqrt(whole[:, :1] / 4608.0 + 1e-06)
-    out_ref[...] = (total * scale * gain_ref[...].reshape(1, -1)).astype(jnp.bfloat16)
+        total += parts_in[d - 1].astype(f32)
+        own += parts_in[d - 1, tp].astype(f32)
+    square = jnp.sum(jnp.sum(total * total, axis=0), axis=-1, keepdims=True)
+    scale = lax.rsqrt(square / 4608.0 + 1e-06)
+    out_ref[...] = (own * scale * gain_ref[...].reshape(1, -1)).astype(jnp.bfloat16)
     for d in range(1, 8):
         part(d).wait_send()
-        sq(d).wait_send()
 
 
 def body(

time: 92.9 us -> 89.4 us (0.962)
  Pallas kernels: 92.2 us -> 88.6 us
    pallas_call x1, Pallas kernels: 87.1 us -> 83.6 us  [gather_and_attend(): pl.pallas_call(gather_kernel, out_shape=(jax.ShapeDtypeStruct((4, 4, 1152...]
where the time goes in v7:
time: 89.4 us; the launch traced here: 89.3 us
  Pallas kernels  88.6 us (99%)
    pallas_call x1, Pallas kernels, gather_and_attend(): pl.pallas_call(gather_kernel, out_shape=(jax.ShapeDtypeStruct((4, 4, 1152...  83.6 us
    pallas_call x1, Pallas kernels, write_out(): pl.pallas_call(write_kernel, out_shape=(jax.ShapeDtypeStruct((4608, 1024)...  5.04 us

profile of v7, /device:TPU:1, one launch (start us, length us, event | category | flops | bytes accessed | tf_op | source)
XLA Modules:
  0.0 89.3 jit_solution(9880011404350711166)
XLA Ops:
  0.6 83.6 %gather_and_attend.1 = (bf16[4,4,1152,256]{3,2,1,0:T(8,128)(2,1)S(1)}, bf16[4,4,128,1152]{3,2,1,0:T(8,128)(2,1)S(1)}, bf16[4,576]{1,0:T(4,128)(2,1)S(1)}) custom-call(bf16[32,4608]{1,0:T(8,128)(2,1)} %q_ref.1, bf16[16,4608]{1,0:T(8,128)(2,1)} %k_ref.1, bf16[16,4608]{1,0:T(8,128)(2,1)} %v_ref.1, bf16[36,4096]{1,0:T(8,128)(2,1)} %o_ref.1, ...), custom_call_target="tpu_custom_call" | custom-call | tf_op jit(solution)/shard_map/gather_and_attend/pallas_call | solution.py:333
  84.2 5.0 %write_out.1 = (bf16[4608,1024]{1,0:T(8,128)(2,1)}, bf16[512,4608]{1,0:T(8,128)(2,1)}, bf16[4,576]{1,0:T(4,128)(2,1)}) custom-call(bf16[4,4,1152,256]{3,2,1,0:T(8,128)(2,1)S(1)} %get-tuple-element.6.gq, bf16[4,4,128,1152]{3,2,1,0:T(8,128)(2,1)S(1)} %get-tuple-element.7.go, bf16[4,576]{1,0:T(4,128)(2,1)S(1)} %get-tuple-element.8.small), custom_call_target="tpu_custom_call" | custom-call | tf_op jit(solution)/shard_map/write_out/pallas_call | solution.py:439

commit v8 on v7

--- a/solution.py
+++ b/solution.py
@@ -16,6 +16,10 @@
     return pltpu.make_async_remote_copy(
         src_ref=src, dst_ref=dst, send_sem=ssem, recv_sem=rsem, device_id=device,
         device_id_type=MESH)
+
+
+def settle(ref, sem):
+    pltpu.make_async_copy(ref, ref, sem).wait()
 
 
 def gather_kernel(q_ref, k_ref, v_ref, o_ref, hidden_hbm, gain_hbm, kc_hbm, vc_hbm, pos_hbm, post_hbm,
@@ -60,7 +64,7 @@
         p = (tp + i) % 8
         gd = (g + j) % 4
         src = o_ref.at[:, pl.ds(pl.multiple_of(p * 512 + gd * 128, 128), 128)]
-        return src, s1o.at[slot], place(gd // 2, zdest, gd % 2), p, o_send.at[4 * i + j], o_recv
+        return src, s1o.at[slot], place(gd // 2, zdest, gd % 2), p, o_send, o_recv
 
     def exchange(src, dst, dest_rep, dest_tp, ssem, rsem):
         own = jnp.logical_and(dest_rep == rep, dest_tp == tp)
@@ -72,13 +76,6 @@
         @pl.when(jnp.logical_not(own))
         def _():
             remote(src, dst, ssem, rsem, (dest_rep, dest_tp)).start()
-
-    def exchange_done(src, dst, dest_rep, dest_tp, ssem, rsem):
-        own = jnp.logical_and(dest_rep == rep, dest_tp == tp)
-
-        @pl.when(jnp.logical_not(own))
-        def _():
-            remote(src, dst, ssem, rsem, (dest_rep, dest_tp)).wait_send()
 
     for p in range(8):
         for gd in range(4):
@@ -102,7 +99,7 @@
         row = pl.multiple_of(jnp.where(away, there, row), krows)
         dst = s1a.at[z, pl.ds(row, rows)]
         device = (place(jnp.where(away, to_h, h), zd, core), jnp.where(away, to_tp, tp))
-        return away, src, dst, remote(src, dst, a_send.at[3 * dist + part], a_recv.at[dist], device)
+        return away, src, dst, remote(src, dst, a_send.at[min(dist, 1)], a_recv.at[dist], device)
 
     for dist in (2, 1, 3, 0):
         for part in range(3):
@@ -123,29 +120,29 @@
         copy.wait()
     prepare(pos_ref, hidden_ref, gain_ref, nrm, acc, rope)
 
-    def to_owners(dist, act):
+    def to_owners(dist):
         zs = (tp + dist) % 4
 
-        def message(when, index, row, rows, dest, first, block):
+        def message(when, row, rows, dest, first, block):
             dst = s1q.at[pl.ds(pl.multiple_of(first, rows), rows)]
 
             @pl.when(when)
             def _():
-                act(s1a.at[zs, pl.ds(row, rows)], dst, dest, block, b_send.at[4 * dist + index], q_recv)
+                exchange(s1a.at[zs, pl.ds(row, rows)], dst, dest, block, b_send, q_recv)
 
         y = tp % 4
-        message(jnp.logical_not(last_x), 0, 0, qrows, place(0, z, core), tp * qrows, h * 4 + zs)
-        message(first_x, 1, qrows, qrows, place(0, z, core), (4 + y) * qrows, 4 + zs)
+        message(jnp.logical_not(last_x), 0, qrows, place(0, z, core), tp * qrows, h * 4 + zs)
+        message(first_x, qrows, qrows, place(0, z, core), (4 + y) * qrows, 4 + zs)
         for i in range(2):
-            message(jnp.logical_not(first_x), 1 + i, qrows + i * krows, krows, place(1, z, i),
+            message(jnp.logical_not(first_x), qrows + i * krows, krows, place(1, z, i),
                     core * 128 + tp * krows, h * 4 + zs)
-            message(last_x, 3 * i, i * krows, krows, place(1, z, i), core * 128 + y * krows, zs)
+            message(last_x, i * krows, krows, place(1, z, i), core * 128 + y * krows, zs)
 
     for dist in (0, 2, 1, 3):
         zs = (tp + dist) % 4
         came = s1a.at[zs]
         pltpu.make_async_copy(came, came, a_recv.at[(z + 4 - zs) % 4]).wait()
-        to_owners(dist, exchange)
+        to_owners(dist)
 
     def chunk(a, zs, gs, half):
         return gathered[a].at[zs, gs, pl.ds(half * halves[a], halves[a])]
@@ -163,32 +160,37 @@
 
     def xearly(i):
         c = early_rows(i, g)
-        return remote(c, c, x_send.at[2 + i], x_recv.at[2 + i], (place(1 - h, z, core), tp))
+        return remote(c, c, x_send.at[2], x_recv.at[1 + i], (place(1 - h, z, core), tp))
 
     def dearly(i):
         c = early_rows(i, gpar)
-        return remote(c, c, d_send.at[32 + i], d_recv.at[32 + i], (place(h, z, 1 - core), tp))
+        return remote(c, c, d_send.at[1], d_recv.at[4 + i], (place(h, z, 1 - core), tp))
 
     def d2d(a, xp, s):
         if s < 2:
             c = chunk(a, z, piece_g[xp], s)
         else:
             c = ring_chunk(a, xp, piece_z[s // 2], s % 2)
-        i = (a * 2 + xp) * 8 + s
-        return remote(c, c, d_send.at[i], d_recv.at[i], (place(h, z, 1 - core), tp))
+        i = a * 2 + xp
+        return remote(c, c, d_send.at[i], d_recv.at[i * 4 + s // 2], (place(h, z, 1 - core), tp))
+
+    def d2d_piece_done(a, xp, i):
+        settle(gathered[a].at[piece_z[i], 0], d_recv.at[(a * 2 + xp) * 4 + i])
 
     up = (place(h, zp, core), tp)
     down = (place(h, zm, core), tp)
+
+    ring = {(1, 0): 0, (0, 0): 1, (0, 1): 2}
 
     def zcopy(a, xp, i):
         zs, half, to = ((z, 0, up), (z, 1, up), (z, 0, down), (z, 1, down), (zm, 0, up), (zp, 1, down))[i]
         c = ring_chunk(a, xp, zs, half)
-        j = (a * 2 + xp) * 6 + i
-        return remote(c, c, z_send.at[j], z_recv.at[j], to)
+        j = ring[a, xp]
+        return remote(c, c, z_send.at[j], z_recv.at[j * 6 + i], to)
 
     def xcopy(a, s):
         c = chunk(a, piece_z[s // 2], g, s % 2)
-        return remote(c, c, x_send.at[a * 8 + s], x_recv.at[a * 8 + s], (place(1 - h, z, core), tp))
+        return remote(c, c, x_send.at[a], x_recv.at[a * 5 + s], (place(1 - h, z, core), tp))
 
     def arrived(a, xp, s):
         d2d(a, xp, s).start()
@@ -224,15 +226,22 @@
     for b in range(9):
         go[z, g, :, b * 128:(b + 1) * 128] = so[b * 128:(b + 1) * 128, :].T.astype(jnp.bfloat16)
     launch(1, 0)
-    for dist in range(4):
-        to_owners(dist, exchange_done)
+    for s in range(2):
+        xcopy(1, s).start()
+    def slices_left(when, rows):
+        @pl.when(when)
+        def _():
+            settle(s1q.at[pl.ds(0, rows)], b_send)
+
+    ends = jnp.logical_or(first_x, last_x)
+    slices_left(first_x, s1q.shape[0] - qrows)
+    slices_left(last_x, s1q.shape[0] - krows)
+    slices_left(jnp.logical_not(ends), s1q.shape[0])
     for i in range(1, 8):
         peer = (2 * h + lo + i // 2) % 4
         pl.semaphore_signal(
             row_sem, inc=1, device_id_type=MESH,
             device_id=(place(peer // 2, z, (core + i) % 2), (peer % 2) * 4 + tp % 4))
-    for s in range(2):
-        xcopy(1, s).start()
     pltpu.make_async_copy(s1q, s1q, q_recv).wait()
     for b in range(9):
         for c in range(2):
@@ -262,10 +271,7 @@
             acc[gs] += jnp.dot(nrm[piece_z[i]], gq[piece_z[i], gs], preferred_element_type=jnp.float32)
 
         add(piece_g[xp])
-        for s in (2 * i, 2 * i + 1):
-            d2d(0, xp, s).wait_recv()
-        if xp == 1 and i > 0:
-            dearly(i).wait_recv()
+        d2d_piece_done(0, xp, i)
         add(piece_g[xp] + 1 - 2 * core)
 
     for i in range(4):
@@ -288,38 +294,50 @@
         xcopy(1, s).wait_recv()
         d2d(1, 1, s).start()
     att = attention(pos_ref, kc, vc, acc, rope)
-    for xp in range(2):
-        for s in range(8):
-            d2d(1, xp, s).wait_recv()
-    for zs in range(4):
-        part = jnp.dot(att, go[zs].reshape(512, 1152), preferred_element_type=jnp.float32)
-        part = part.astype(jnp.bfloat16)
-        part_ref[2 * WO_SLICE[zs]] = part[:, :576]
-        part_ref[2 * WO_SLICE[zs] + 1] = part[:, 576:]
-    sum_and_norm(part_ref, post_ref, out_ref, parts_in, p_send, p_recv)
-    for part in range(3):
-        for dist in range(4):
-            away, _, _, copy = along_z(dist, part)
-            if dist == 0:
-                pl.when(away)(copy.wait_send)
-            else:
-                copy.wait_send()
-    for p in range(8):
-        for gd in range(4):
-            exchange_done(*o_slice(p, gd))
-    for s in range(2):
-        xcopy(0, s).wait_send()
-    for s in range(8):
-        xcopy(1, s).wait_send()
-    for i in range(1, 4):
-        xearly(i).wait_send()
-        dearly(i).wait_send()
-    for a, xp in ((1, 0), (0, 0), (1, 1), (0, 1)):
-        if (a, xp) != (1, 1):
-            for i in range(6):
-                zcopy(a, xp, i).wait_send()
-        for s in range(8):
-            d2d(a, xp, s).wait_send()
+    def part_slices(i):
+        zs = piece_z[i]
+        j = jnp.where(zs == 0, 0, jnp.where(zs == 3, 1, zs + 1))
+        return pl.ds(2 * j, 2)
+
+    def part(i, d):
+        return remote(part_ref.at[part_slices(i)], parts_in.at[d - 1, part_slices(i)],
+                      p_send, p_recv, (rep, (tp + d) % 8))
+
+    for i in range(4):
+        for xp in range(2):
+            d2d_piece_done(1, xp, i)
+        both = jnp.dot(att, go[piece_z[i]].reshape(512, 1152), preferred_element_type=jnp.float32)
+        both = both.astype(jnp.bfloat16)
+        first = part_slices(i).start
+        part_ref[first] = both[:, :576]
+        part_ref[first + 1] = both[:, 576:]
+        for d in (6, 2, 5, 7, 1, 3, 4):
+            part(i, d).start()
+    settle(parts_in, p_recv)
+    sum_and_norm(part_ref, post_ref, out_ref, parts_in)
+    settle(parts_in, p_send)
+    settle(s1a.at[pl.ds(0, 3)], a_send.at[1])
+
+    @pl.when(ends)
+    def _():
+        settle(s1a.at[0, pl.ds(0, qrows)], a_send.at[0])
+
+    @pl.when(zdest == z)
+    def _():
+        settle(s1o.at[pl.ds(0, 31)], o_send)
+
+    @pl.when(zdest != z)
+    def _():
+        settle(s1o, o_send)
+
+    settle(go.at[0, pl.ds(0, 3)], z_send.at[0])
+    settle(gq.at[0, pl.ds(0, 3)], z_send.at[1])
+    settle(gq.at[0, pl.ds(0, 3), pl.ds(0, 2 * late)], z_send.at[2])
+    settle(gq.at[0, 0], x_send.at[0])
+    settle(go.at[0], x_send.at[1])
+    settle(gq.at[0, pl.ds(0, 3), pl.ds(0, early)], x_send.at[2])
+    for i in range(4):
+        settle(gathered[i // 2].at[0], d_send.at[i])
 
 
 def in_hbm(x):
@@ -344,9 +362,8 @@
             vmem((8, 4, 576), bf), vmem((7, 8, 4, 576), bf),
             vmem((4, 64, 1152), bf), vmem((256, 1152), bf), vmem((32, 36, 128), bf),
             vmem((1152, 128), f32),
-            dma((12,)), dma((4,)), dma((16,)), dma, dma((32,)), dma,
-            dma((24,)), dma((24,)), dma((16,)), dma((16,)), dma((36,)), dma((36,)),
-            pltpu.SemaphoreType.REGULAR, dma((6,)), dma((7,)), dma((7,)),
+            dma((2,)), dma((4,)), dma, dma, dma, dma, dma((3,)), dma((18,)), dma((3,)), dma((13,)),
+            dma((4,)), dma((16,)), pltpu.SemaphoreType.REGULAR, dma((6,)), dma, dma,
         ],
         compiler_params=pltpu.CompilerParams(
             has_side_effects=True, collective_id=0, vmem_limit_bytes=16 * 1024 * 1024),
@@ -448,28 +465,17 @@
     )(gq, go, small)
 
 
-def sum_and_norm(part_ref, gain_ref, out_ref, parts_in, p_send, p_recv):
+def sum_and_norm(part_ref, gain_ref, out_ref, parts_in):
     f32 = jnp.float32
-    rep = lax.axis_index("rep")
     tp = lax.axis_index("tp")
-
-    def part(d):
-        return remote(part_ref, parts_in.at[d - 1], p_send.at[d - 1], p_recv.at[d - 1],
-                      (rep, (tp + d) % 8))
-
-    for d in (6, 2, 5, 7, 1, 3, 4):
-        part(d).start()
     total = part_ref[...].astype(f32)
     own = part_ref[tp].astype(f32)
-    for d in (4, 1, 3, 7, 5, 2, 6):
-        part(d).wait_recv()
-        total += parts_in[d - 1].astype(f32)
-        own += parts_in[d - 1, tp].astype(f32)
+    for d in range(7):
+        total += parts_in[d].astype(f32)
+        own += parts_in[d, tp].astype(f32)
     square = jnp.sum(jnp.sum(total * total, axis=0), axis=-1, keepdims=True)
     scale = lax.rsqrt(square / 4608.0 + 1e-06)
     out_ref[...] = (own * scale * gain_ref[...].reshape(1, -1)).astype(jnp.bfloat16)
-    for d in range(1, 8):
-        part(d).wait_send()
 
 
 def body(

time: 89.4 us -> 87.2 us (0.975)
  Pallas kernels: 88.6 us -> 86.3 us
    pallas_call x1, Pallas kernels: 83.6 us -> 81.2 us  [gather_and_attend(): pl.pallas_call(gather_kernel, out_shape=(jax.ShapeDtypeStruct((4, 4, 1152...]
where the time goes in v8:
time: 87.2 us; the launch traced here: 86.9 us
  Pallas kernels  86.3 us (99%)
    pallas_call x1, Pallas kernels, gather_and_attend(): pl.pallas_call(gather_kernel, out_shape=(jax.ShapeDtypeStruct((4, 4, 1152...  81.2 us
    pallas_call x1, Pallas kernels, write_out(): pl.pallas_call(write_kernel, out_shape=(jax.ShapeDtypeStruct((4608, 1024)...  5.04 us

profile of v8, /device:TPU:1, one launch (start us, length us, event | category | flops | bytes accessed | tf_op | source)
XLA Modules:
  0.0 86.9 jit_solution(16328490423062723017)
XLA Ops:
  0.6 81.2 %gather_and_attend.1 = (bf16[4,4,1152,256]{3,2,1,0:T(8,128)(2,1)S(1)}, bf16[4,4,128,1152]{3,2,1,0:T(8,128)(2,1)S(1)}, bf16[4,576]{1,0:T(4,128)(2,1)S(1)}) custom-call(bf16[32,4608]{1,0:T(8,128)(2,1)} %q_ref.1, bf16[16,4608]{1,0:T(8,128)(2,1)} %k_ref.1, bf16[16,4608]{1,0:T(8,128)(2,1)} %v_ref.1, bf16[36,4096]{1,0:T(8,128)(2,1)} %o_ref.1, ...), custom_call_target="tpu_custom_call" | custom-call | tf_op jit(solution)/shard_map/gather_and_attend/pallas_call | solution.py:351
  81.9 5.0 %write_out.1 = (bf16[4608,1024]{1,0:T(8,128)(2,1)}, bf16[512,4608]{1,0:T(8,128)(2,1)}, bf16[4,576]{1,0:T(4,128)(2,1)}) custom-call(bf16[4,4,1152,256]{3,2,1,0:T(8,128)(2,1)S(1)} %get-tuple-element.6.gq, bf16[4,4,128,1152]{3,2,1,0:T(8,128)(2,1)S(1)} %get-tuple-element.7.go, bf16[4,576]{1,0:T(4,128)(2,1)S(1)} %get-tuple-element.8.small), custom_call_target="tpu_custom_call" | custom-call | tf_op jit(solution)/shard_map/write_out/pallas_call | solution.py:456

commit v9 on v8

--- a/solution.py
+++ b/solution.py
@@ -66,7 +66,10 @@
         src = o_ref.at[:, pl.ds(pl.multiple_of(p * 512 + gd * 128, 128), 128)]
         return src, s1o.at[slot], place(gd // 2, zdest, gd % 2), p, o_send, o_recv
 
-    def exchange(src, dst, dest_rep, dest_tp, ssem, rsem):
+    def exchange(first, src, dst, dest_rep, dest_tp, ssem, rsem):
+        if not first:
+            remote(src, dst, ssem, rsem, (dest_rep, dest_tp)).start()
+            return
         own = jnp.logical_and(dest_rep == rep, dest_tp == tp)
 
         @pl.when(own)
@@ -79,7 +82,7 @@
 
     for p in range(8):
         for gd in range(4):
-            exchange(*o_slice(p, gd))
+            exchange(p == 0 and gd == 0, *o_slice(p, gd))
 
     width = s1q.shape[1]
     qrows, krows = q_ref.shape[0], k_ref.shape[0]
@@ -128,7 +131,7 @@
 
             @pl.when(when)
             def _():
-                exchange(s1a.at[zs, pl.ds(row, rows)], dst, dest, block, b_send, q_recv)
+                exchange(dist == 0, s1a.at[zs, pl.ds(row, rows)], dst, dest, block, b_send, q_recv)
 
         y = tp % 4
         message(jnp.logical_not(last_x), 0, qrows, place(0, z, core), tp * qrows, h * 4 + zs)
@@ -147,7 +150,7 @@
     def chunk(a, zs, gs, half):
         return gathered[a].at[zs, gs, pl.ds(half * halves[a], halves[a])]
 
-    early = 192
+    early = 128
     late = (gq.shape[2] - early) // 2
 
     def ring_chunk(a, xp, zs, half):
@@ -201,13 +204,15 @@
         arrived(a, xp, 0)
         arrived(a, xp, 1)
 
-    def relay(a, xp):
+    def forward(a, xp):
         zcopy(a, xp, 0).wait_recv()
         zcopy(a, xp, 4).start()
         arrived(a, xp, 2)
         zcopy(a, xp, 3).wait_recv()
         zcopy(a, xp, 5).start()
         arrived(a, xp, 5)
+
+    def take(a, xp):
         zcopy(a, xp, 1).wait_recv()
         arrived(a, xp, 3)
         zcopy(a, xp, 2).wait_recv()
@@ -242,6 +247,7 @@
         pl.semaphore_signal(
             row_sem, inc=1, device_id_type=MESH,
             device_id=(place(peer // 2, z, (core + i) % 2), (peer % 2) * 4 + tp % 4))
+    forward(1, 0)
     pltpu.make_async_copy(s1q, s1q, q_recv).wait()
     for b in range(9):
         for c in range(2):
@@ -251,10 +257,11 @@
     pl.semaphore_wait(row_sem, 7)
     for s in range(2):
         xcopy(0, s).start()
-    relay(1, 0)
+    take(1, 0)
     for s in (2, 5, 3, 4):
         xcopy(1, s).start()
-    relay(0, 0)
+    forward(0, 0)
+    take(0, 0)
     for i in (1, 2):
         xearly(i).start()
     for s in range(2):
@@ -276,7 +283,8 @@
 
     for i in range(4):
         project(0, i)
-    relay(0, 1)
+    forward(0, 1)
+    take(0, 1)
     project(1, 0)
     for s in (0, 1, 2, 5, 3, 4):
         xcopy(1, s).wait_recv()

time: 87.2 us -> 85.8 us (0.984)
  Pallas kernels: 86.3 us -> 85.1 us
    pallas_call x1, Pallas kernels: 81.2 us -> 80 us  [gather_and_attend(): pl.pallas_call(gather_kernel, out_shape=(jax.ShapeDtypeStruct((4, 4, 1152...]
where the time goes in v9:
time: 85.8 us; the launch traced here: 85.7 us
  Pallas kernels  85.1 us (99%)
    pallas_call x1, Pallas kernels, gather_and_attend(): pl.pallas_call(gather_kernel, out_shape=(jax.ShapeDtypeStruct((4, 4, 1152...  80 us
    pallas_call x1, Pallas kernels, write_out(): pl.pallas_call(write_kernel, out_shape=(jax.ShapeDtypeStruct((4608, 1024)...  5.04 us

profile of v9, /device:TPU:1, one launch (start us, length us, event | category | flops | bytes accessed | tf_op | source)
XLA Modules:
  0.0 85.7 jit_solution(996669344691315280)
XLA Ops:
  0.6 80.0 %gather_and_attend.1 = (bf16[4,4,1152,256]{3,2,1,0:T(8,128)(2,1)S(1)}, bf16[4,4,128,1152]{3,2,1,0:T(8,128)(2,1)S(1)}, bf16[4,576]{1,0:T(4,128)(2,1)S(1)}) custom-call(bf16[32,4608]{1,0:T(8,128)(2,1)} %q_ref.1, bf16[16,4608]{1,0:T(8,128)(2,1)} %k_ref.1, bf16[16,4608]{1,0:T(8,128)(2,1)} %v_ref.1, bf16[36,4096]{1,0:T(8,128)(2,1)} %o_ref.1, ...), custom_call_target="tpu_custom_call" | custom-call | tf_op jit(solution)/shard_map/gather_and_attend/pallas_call | solution.py:359
  80.7 5.0 %write_out.1 = (bf16[4608,1024]{1,0:T(8,128)(2,1)}, bf16[512,4608]{1,0:T(8,128)(2,1)}, bf16[4,576]{1,0:T(4,128)(2,1)}) custom-call(bf16[4,4,1152,256]{3,2,1,0:T(8,128)(2,1)S(1)} %get-tuple-element.6.gq, bf16[4,4,128,1152]{3,2,1,0:T(8,128)(2,1)S(1)} %get-tuple-element.7.go, bf16[4,576]{1,0:T(4,128)(2,1)S(1)} %get-tuple-element.8.small), custom_call_target="tpu_custom_call" | custom-call | tf_op jit(solution)/shard_map/write_out/pallas_call | solution.py:464

commit v10 on v9

--- a/solution.py
+++ b/solution.py
@@ -167,18 +167,18 @@
 
     def dearly(i):
         c = early_rows(i, gpar)
-        return remote(c, c, d_send.at[1], d_recv.at[4 + i], (place(h, z, 1 - core), tp))
+        return remote(c, c, d_send.at[0], d_recv.at[4 + i], (place(h, z, 1 - core), tp))
 
     def d2d(a, xp, s):
         if s < 2:
             c = chunk(a, z, piece_g[xp], s)
         else:
             c = ring_chunk(a, xp, piece_z[s // 2], s % 2)
-        i = a * 2 + xp
-        return remote(c, c, d_send.at[i], d_recv.at[i * 4 + s // 2], (place(h, z, 1 - core), tp))
-
-    def d2d_piece_done(a, xp, i):
-        settle(gathered[a].at[piece_z[i], 0], d_recv.at[(a * 2 + xp) * 4 + i])
+        i = s // 2 + (8 if a else 4 * xp)
+        return remote(c, c, d_send.at[a], d_recv.at[i], (place(h, z, 1 - core), tp))
+
+    def d2d_piece_done(xp, i):
+        settle(gq.at[piece_z[i], 0], d_recv.at[4 * xp + i])
 
     up = (place(h, zp, core), tp)
     down = (place(h, zm, core), tp)
@@ -278,7 +278,7 @@
             acc[gs] += jnp.dot(nrm[piece_z[i]], gq[piece_z[i], gs], preferred_element_type=jnp.float32)
 
         add(piece_g[xp])
-        d2d_piece_done(0, xp, i)
+        d2d_piece_done(xp, i)
         add(piece_g[xp] + 1 - 2 * core)
 
     for i in range(4):
@@ -312,8 +312,7 @@
                       p_send, p_recv, (rep, (tp + d) % 8))
 
     for i in range(4):
-        for xp in range(2):
-            d2d_piece_done(1, xp, i)
+        settle(go.at[piece_z[i], pl.ds(0, 2)], d_recv.at[8 + i])
         both = jnp.dot(att, go[piece_z[i]].reshape(512, 1152), preferred_element_type=jnp.float32)
         both = both.astype(jnp.bfloat16)
         first = part_slices(i).start
@@ -344,8 +343,8 @@
     settle(gq.at[0, 0], x_send.at[0])
     settle(go.at[0], x_send.at[1])
     settle(gq.at[0, pl.ds(0, 3), pl.ds(0, early)], x_send.at[2])
-    for i in range(4):
-        settle(gathered[i // 2].at[0], d_send.at[i])
+    for i in range(2):
+        settle(gathered[i].at[pl.ds(0, 2)], d_send.at[i])
 
 
 def in_hbm(x):
@@ -371,7 +370,7 @@
             vmem((4, 64, 1152), bf), vmem((256, 1152), bf), vmem((32, 36, 128), bf),
             vmem((1152, 128), f32),
             dma((2,)), dma((4,)), dma, dma, dma, dma, dma((3,)), dma((18,)), dma((3,)), dma((13,)),
-            dma((4,)), dma((16,)), pltpu.SemaphoreType.REGULAR, dma((6,)), dma, dma,
+            dma((2,)), dma((12,)), pltpu.SemaphoreType.REGULAR, dma((6,)), dma, dma,
         ],
         compiler_params=pltpu.CompilerParams(
             has_side_effects=True, collective_id=0, vmem_limit_bytes=16 * 1024 * 1024),

time: 85.8 us -> 85.8 us (level)
  no operation moved by 1% of the time
where the time goes in v10:
time: 85.8 us; the launch traced here: 85.7 us
  Pallas kernels  85 us (99%)
    pallas_call x1, Pallas kernels, gather_and_attend(): pl.pallas_call(gather_kernel, out_shape=(jax.ShapeDtypeStruct((4, 4, 1152...  80 us
    pallas_call x1, Pallas kernels, write_out(): pl.pallas_call(write_kernel, out_shape=(jax.ShapeDtypeStruct((4608, 1024)...  5.04 us

profile of v10, /device:TPU:1, one launch (start us, length us, event | category | flops | bytes accessed | tf_op | source)
XLA Modules:
  0.0 85.7 jit_solution(10014436597717647495)
XLA Ops:
  0.6 80.0 %gather_and_attend.1 = (bf16[4,4,1152,256]{3,2,1,0:T(8,128)(2,1)S(1)}, bf16[4,4,128,1152]{3,2,1,0:T(8,128)(2,1)S(1)}, bf16[4,576]{1,0:T(4,128)(2,1)S(1)}) custom-call(bf16[32,4608]{1,0:T(8,128)(2,1)} %q_ref.1, bf16[16,4608]{1,0:T(8,128)(2,1)} %k_ref.1, bf16[16,4608]{1,0:T(8,128)(2,1)} %v_ref.1, bf16[36,4096]{1,0:T(8,128)(2,1)} %o_ref.1, ...), custom_call_target="tpu_custom_call" | custom-call | tf_op jit(solution)/shard_map/gather_and_attend/pallas_call | solution.py:358
  80.6 5.0 %write_out.1 = (bf16[4608,1024]{1,0:T(8,128)(2,1)}, bf16[512,4608]{1,0:T(8,128)(2,1)}, bf16[4,576]{1,0:T(4,128)(2,1)}) custom-call(bf16[4,4,1152,256]{3,2,1,0:T(8,128)(2,1)S(1)} %get-tuple-element.6.gq, bf16[4,4,128,1152]{3,2,1,0:T(8,128)(2,1)S(1)} %get-tuple-element.7.go, bf16[4,576]{1,0:T(4,128)(2,1)S(1)} %get-tuple-element.8.small), custom_call_target="tpu_custom_call" | custom-call | tf_op jit(solution)/shard_map/write_out/pallas_call | solution.py:463
